TPU v7x, 32 devices: a whole 2x2x4 slice. The times are simulated.
32 devices in a mesh: expert: 8 (over z, y), shard: 4 (over x, core).
Axes of the slice: x: 2, y: 2, z: 4, core: 2. Of those that a mesh axis runs over, the one named last changes fastest.
Arguments:
- tokens: bfloat16 [4096, 2048], P(('expert', 'shard')), may hold values from -6 to 6
- gain_attn: float32 [2048], replicated, may hold values from 0.1 to 1.9
- w_qkv: bfloat16 [3, 2048, 2048], P(None, 'expert', 'shard'), may hold values from -0.125 to 0.125
- b_qkv: float32 [3, 2048], P(None, 'shard'), may hold values from -9 to 9, as said below
- w_out: bfloat16 [2048, 2048], P('shard', 'expert'), may hold values from -0.5 to 0.5
- gain_ffn: float32 [2048], replicated, may hold values from 0.1 to 1.9
- w_router: bfloat16 [2048, 32], replicated, may hold values from -0.125 to 0.125
- shared_gate: float32 [2048], replicated, may hold values from -0.125 to 0.125
- w_shared_gu: bfloat16 [2, 2048, 5632], P(None, 'expert', 'shard'), may hold values from -0.125 to 0.125
- w_shared_down: bfloat16 [5632, 2048], P('shard', 'expert'), may hold values from -0.078125 to 0.078125
- w_expert_gu: bfloat16 [32, 2, 2048, 1408], P(('expert', 'shard')), may hold values from -0.125 to 0.125
- w_expert_down: bfloat16 [32, 1408, 2048], P(('expert', 'shard')), may hold values from -1.25 to 1.25
- routes: int32 [4096, 4], P(('expert', 'shard')), may hold values from 0 to 31, all different within a row; in each aligned block of 128 rows (0 to 127, 128 to 255, ...) at most 32 rows name the same one
- grad_out: bfloat16 [4096, 2048], P(('expert', 'shard')), may hold values from -6 to 6
Outputs:
- result: bfloat16 [4096, 2048], P(('expert', 'shard'))
- grad_tokens: float32 [4096, 2048], P(('expert', 'shard'))
- grad_gain_attn: float32 [2048], replicated
- grad_w_qkv: float32 [3, 2048, 2048], P(None, 'expert', 'shard')
- grad_b_qkv: float32 [3, 2048], replicated
- grad_w_out: float32 [2048, 2048], P('shard', 'expert')
- grad_gain_ffn: float32 [2048], replicated
- grad_w_router: float32 [2048, 32], replicated
- grad_shared_gate: float32 [2048], replicated
- grad_w_shared_gu: float32 [2, 2048, 5632], P(None, 'expert', 'shard')
- grad_w_shared_down: float32 [5632, 2048], P('shard', 'expert')
- grad_w_expert_gu: float32 [32, 2, 2048, 1408], P(('expert', 'shard'))
- grad_w_expert_down: float32 [32, 1408, 2048], P(('expert', 'shard'))
Inputs may be any that keep to these rules, and one draw needn't show every extreme that they name: `routes`: each row names 4 different experts; among the rows of one device no expert is named more than 32 times, a bound that some block reaches. `b_qkv`: biases of the queries, keys and values.
All inputs are finite; a program needn't handle non-finite values.
Results may differ from a plain program's by a relative error of at most 0.018.
The roundings to bfloat16 on the way count: a program that leaves them out, or rounds other values in their place, can miss the bound.
Values may be sent and summed in bfloat16 or wider, within the bound.
A program may use at most 384 MiB of HBM per device.

v0:
```python
import jax
import jax.numpy as jnp
from jax import lax
from jax.sharding import PartitionSpec as P

HEAD_DIM = 128
TOPK = 4


eps = 1e-06
rope_base = 1000000.0
highest = lax.Precision.HIGHEST


def rope_tables(length, head_width):
    half_width = head_width // 2
    inverse = rope_base ** (-(jnp.arange(half_width, dtype=jnp.float32) * 2.0 / head_width))
    angles = jnp.arange(length, dtype=jnp.float32)[:, None] * inverse[None, :]
    angles = jnp.concatenate([angles, angles], axis=1)
    return (jnp.cos(angles), jnp.sin(angles))


def rotate(values, cosine, sine_tab):
    half_width = values.shape[-1] // 2
    turned = jnp.concatenate([-values[..., half_width:], values[..., :half_width]], axis=-1)
    return values * cosine[:, None, :] + turned * sine_tab[:, None, :]


def rotate_back(grad_vals, cosine, sine_tab):
    half_width = grad_vals.shape[-1] // 2
    scaled = grad_vals * sine_tab[:, None, :]
    turned = jnp.concatenate([scaled[..., half_width:], -scaled[..., :half_width]], axis=-1)
    return grad_vals * cosine[:, None, :] + turned


def norm_rows(values):
    scale_rows = lax.rsqrt(jnp.mean(values * values, axis=-1, keepdims=True) + eps)
    return (values * scale_rows, scale_rows)


def norm_back(grad_normed, unit_rows, scale_rows, gain_vec):
    inner_term = grad_normed * gain_vec
    return scale_rows * (
        inner_term - unit_rows * jnp.mean(inner_term * unit_rows, axis=-1, keepdims=True)
    )


def masked_scores(query_blk, keys_low, first_row, factor):
    scores = (
        jnp.einsum("qhd,khd->hqk", query_blk, keys_low, preferred_element_type=jnp.float32) * factor
    )
    row_ids = first_row + jnp.arange(query_blk.shape[0], dtype=jnp.int32)
    col_ids = jnp.arange(keys_low.shape[0], dtype=jnp.int32)
    causal = col_ids[None, :] <= row_ids[:, None]
    return jnp.where(causal[None], scores, -jnp.inf)


def silu_pair(gate_up):
    sig_gate = jax.nn.sigmoid(gate_up[0])
    return (gate_up[0] * sig_gate, sig_gate)


def swiglu_back(grad_hid, gate_up):
    silu_gate, sig_gate = silu_pair(gate_up)
    grad_gate = grad_hid * gate_up[1] * sig_gate * (1.0 + gate_up[0] * (1.0 - sig_gate))
    grad_up = grad_hid * silu_gate
    return jnp.stack([grad_gate, grad_up], axis=0).astype(jnp.bfloat16)


def local(
    tokens,
    gain_attn,
    w_qkv,
    b_qkv,
    w_out,
    gain_ffn,
    w_router,
    shared_gate,
    w_shared_gu,
    w_shared_down,
    w_expert_gu,
    w_expert_down,
    routes,
    grad_out,
):
    own_rows, model_width = tokens.shape
    shard_count = lax.axis_size("shard")
    shard_pos = lax.axis_index("shard")
    seq_len = own_rows * shard_count
    local_width = w_qkv.shape[2]
    local_heads = local_width // HEAD_DIM
    experts_all = w_router.shape[1]
    capacity = 2 * own_rows * TOPK // experts_all
    block_rows = min(512, seq_len)
    block_count = seq_len // block_rows
    factor = HEAD_DIM ** (-0.5)
    first_own = shard_pos * own_rows

    def route_rows(block):
        return lax.all_to_all(block, ("expert", "shard"), split_axis=0, concat_axis=0, tiled=True)

    full_qkv, full_out, full_sgu, full_sdown = (
        lax.all_gather(w_qkv, "expert", axis=1, tiled=True),
        lax.all_gather(w_out, "expert", axis=1, tiled=True),
        lax.all_gather(w_shared_gu, "expert", axis=1, tiled=True),
        lax.all_gather(w_shared_down, "expert", axis=1, tiled=True),
    )
    x_own = tokens.astype(jnp.float32)
    unit_one, scale_one = norm_rows(x_own)
    normed_one = (unit_one * gain_attn).astype(jnp.bfloat16)
    x_group, normed_group = (
        lax.all_gather(tokens, "shard", axis=0, tiled=True),
        lax.all_gather(normed_one, "shard", axis=0, tiled=True),
    )
    projected = (
        jnp.einsum("sd,cdh->csh", normed_group, full_qkv, preferred_element_type=jnp.float32)
        + b_qkv[:, None, :]
    )
    cosine, sine_tab = rope_tables(seq_len, HEAD_DIM)
    split_proj = projected.reshape(3, seq_len, local_heads, HEAD_DIM)
    queries = rotate(split_proj[0], cosine, sine_tab).astype(jnp.bfloat16)
    keys_low = rotate(split_proj[1], cosine, sine_tab).astype(jnp.bfloat16)
    values = split_proj[2].astype(jnp.bfloat16)

    def attn_block(block_id):
        first_row = block_id * block_rows
        scores = masked_scores(queries, keys_low, first_row, factor)
        row_max = jnp.max(scores, axis=-1, keepdims=True)
        weights = jnp.exp(scores - row_max)
        row_sum = jnp.sum(weights, axis=-1, keepdims=True)
        probs_low = (weights / row_sum).astype(jnp.bfloat16)
        mixed_blk = jnp.einsum(
            "hqk,khd->qhd", probs_low, values, preferred_element_type=jnp.float32
        ).astype(jnp.bfloat16)
        return (mixed_blk, (row_max + jnp.log(row_sum))[..., 0])

    mixed_blocks, logsum = lax.map(attn_block, jnp.arange(block_count, dtype=jnp.int32))
    mixed_heads = mixed_blocks.reshape(seq_len, local_width)
    attn_part = jnp.dot(mixed_heads, full_out, preferred_element_type=jnp.float32)
    attn_group = lax.psum(attn_part, "shard")
    hidden_group = x_group.astype(jnp.float32) + attn_group
    unit_two, scale_two = norm_rows(hidden_group)
    normed_two = (unit_two * gain_ffn).astype(jnp.bfloat16)
    gate_logit = jnp.einsum(
        "sd,d->s", normed_two, shared_gate, precision=highest, preferred_element_type=jnp.float32
    )
    gate_sig = jax.nn.sigmoid(gate_logit)
    shared_gu = jnp.einsum("sd,cdf->csf", normed_two, full_sgu, preferred_element_type=jnp.float32)
    shared_silu, shared_sig = silu_pair(shared_gu)
    shared_hid = (shared_silu * shared_gu[1]).astype(jnp.bfloat16)
    shared_part = jnp.dot(shared_hid, full_sdown, preferred_element_type=jnp.float32)
    shared_own = lax.psum_scatter(
        shared_part.astype(jnp.bfloat16), "shard", scatter_dimension=0, tiled=True
    ).astype(jnp.float32)
    normed_own = lax.dynamic_slice_in_dim(normed_two, first_own, own_rows, 0)
    sig_own = lax.dynamic_slice_in_dim(gate_sig, first_own, own_rows, 0)
    hidden_own = lax.dynamic_slice_in_dim(hidden_group, first_own, own_rows, 0)
    router_logits = jnp.dot(normed_own, w_router, preferred_element_type=jnp.float32)
    router_exp = jnp.exp(router_logits)
    router_probs = router_exp / jnp.sum(router_exp, axis=-1, keepdims=True)
    expert_ids = jnp.arange(experts_all, dtype=jnp.int32)
    route_hits = (routes[:, :, None] == expert_ids[None, None, :]).astype(jnp.float32)
    picked = jnp.sum(router_probs[:, None, :] * route_hits, axis=-1)
    flat_routes = routes.reshape(-1)
    matches = (flat_routes[:, None] == expert_ids[None, :]).astype(jnp.int32)
    ranks = jnp.sum((jnp.cumsum(matches, axis=0) - 1) * matches, axis=1)
    targets = flat_routes * capacity + ranks
    send_rows = (
        jnp.zeros((experts_all * capacity, model_width), jnp.bfloat16)
        .at[targets]
        .set(jnp.repeat(normed_own, TOPK, axis=0))
    )
    received = route_rows(send_rows.reshape(experts_all, capacity, model_width)).reshape(
        -1, model_width
    )
    expert_gu = jnp.einsum(
        "rd,cdf->crf", received, w_expert_gu[0], preferred_element_type=jnp.float32
    )
    expert_silu, expert_sig = silu_pair(expert_gu)
    expert_hid = (expert_silu * expert_gu[1]).astype(jnp.bfloat16)
    expert_out = jnp.dot(expert_hid, w_expert_down[0], preferred_element_type=jnp.float32).astype(
        jnp.bfloat16
    )
    returned = route_rows(expert_out.reshape(experts_all, capacity, model_width)).reshape(
        -1, model_width
    )
    route_out = returned[targets].reshape(own_rows, TOPK, model_width)
    routed_own = jnp.sum(route_out.astype(jnp.float32) * picked[:, :, None], axis=1)
    result = (hidden_own + sig_own[:, None] * shared_own + routed_own).astype(jnp.bfloat16)
    grad_own = grad_out.astype(jnp.float32)
    route_grad = (
        (picked[:, :, None] * grad_own[:, None, :]).reshape(-1, model_width).astype(jnp.bfloat16)
    )
    send_grads = (
        jnp.zeros((experts_all * capacity, model_width), jnp.bfloat16).at[targets].set(route_grad)
    )
    grad_recv = route_rows(send_grads.reshape(experts_all, capacity, model_width)).reshape(
        -1, model_width
    )
    grad_expert_down = jnp.einsum(
        "rf,rd->fd", expert_hid, grad_recv, preferred_element_type=jnp.float32
    )
    grad_expert_hid = jnp.einsum(
        "rd,fd->rf", grad_recv, w_expert_down[0], preferred_element_type=jnp.float32
    )
    expert_dgu = swiglu_back(grad_expert_hid, expert_gu)
    grad_expert_gu = jnp.einsum(
        "rd,crf->cdf", received, expert_dgu, preferred_element_type=jnp.float32
    )
    expert_din = jnp.einsum(
        "crf,cdf->rd", expert_dgu, w_expert_gu[0], preferred_element_type=jnp.float32
    ).astype(jnp.bfloat16)
    din_back = route_rows(expert_din.reshape(experts_all, capacity, model_width)).reshape(
        -1, model_width
    )
    grad_normed_own = jnp.sum(
        din_back[targets].reshape(own_rows, TOPK, model_width).astype(jnp.float32), axis=1
    )
    grad_picked = jnp.sum(route_out.astype(jnp.float32) * grad_own[:, None, :], axis=-1)
    grad_router_probs = jnp.sum(grad_picked[:, :, None] * route_hits, axis=1)
    grad_logits = router_probs * (
        grad_router_probs - jnp.sum(router_probs * grad_router_probs, axis=-1, keepdims=True)
    )
    logits_low = grad_logits.astype(jnp.bfloat16)
    grad_router = jnp.einsum(
        "td,te->de", normed_own, logits_low, preferred_element_type=jnp.float32
    )
    grad_normed_own = grad_normed_own + jnp.einsum(
        "te,de->td", logits_low, w_router, preferred_element_type=jnp.float32
    )
    grad_gate_logit = jnp.sum(grad_own * shared_own, axis=-1) * sig_own * (1.0 - sig_own)
    grad_gate_vec = jnp.einsum(
        "td,t->d",
        normed_own,
        grad_gate_logit,
        precision=highest,
        preferred_element_type=jnp.float32,
    )
    grad_normed_own = grad_normed_own + grad_gate_logit[:, None] * shared_gate[None, :]
    grad_group = lax.all_gather(grad_out, "shard", axis=0, tiled=True)
    grad_group_f = grad_group.astype(jnp.float32)
    grad_shared_out = (gate_sig[:, None] * grad_group_f).astype(jnp.bfloat16)
    grad_sdown = jnp.einsum(
        "sf,sd->fd", shared_hid, grad_shared_out, preferred_element_type=jnp.float32
    )
    grad_shared_hid = jnp.einsum(
        "sd,fd->sf", grad_shared_out, full_sdown, preferred_element_type=jnp.float32
    )
    shared_dgu = swiglu_back(grad_shared_hid, shared_gu)
    grad_sgu = jnp.einsum("sd,csf->cdf", normed_two, shared_dgu, preferred_element_type=jnp.float32)
    normed_part = jnp.einsum(
        "csf,cdf->sd", shared_dgu, full_sgu, preferred_element_type=jnp.float32
    )
    own_part = lax.dynamic_slice_in_dim(normed_part, first_own, own_rows, 0) + grad_normed_own
    normed_part = lax.dynamic_update_slice_in_dim(normed_part, own_part, first_own, 0)
    grad_normed_two = lax.psum(normed_part, "shard")
    grad_hidden = grad_group_f + norm_back(grad_normed_two, unit_two, scale_two, gain_ffn)
    grad_gain_two = jnp.sum(
        lax.dynamic_slice_in_dim(grad_normed_two * unit_two, first_own, own_rows, 0), axis=0
    )
    grad_hidden_low = grad_hidden.astype(jnp.bfloat16)
    grad_wout = jnp.einsum(
        "sh,sd->hd", mixed_heads, grad_hidden_low, preferred_element_type=jnp.float32
    )
    grad_mixed = jnp.einsum(
        "sd,hd->sh", grad_hidden_low, full_out, preferred_element_type=jnp.float32
    ).astype(jnp.bfloat16)
    grad_mixed = grad_mixed.reshape(seq_len, local_heads, HEAD_DIM)

    def attn_back(carry_pair, block_id):
        grad_keys, grad_values = carry_pair
        first_row = block_id * block_rows
        scores = masked_scores(queries, keys_low, first_row, factor)
        soft_probs = jnp.exp(scores - logsum[block_id][:, :, None])
        probs_low = soft_probs.astype(jnp.bfloat16)
        grad_values = grad_values + jnp.einsum(
            "hqk,qhd->khd", probs_low, grad_mixed, preferred_element_type=jnp.float32
        )
        grad_probs = jnp.einsum(
            "qhd,khd->hqk", grad_mixed, values, preferred_element_type=jnp.float32
        )
        grad_scores = soft_probs * (
            grad_probs - jnp.sum(soft_probs * grad_probs, axis=-1, keepdims=True)
        )
        scores_low = grad_scores.astype(jnp.bfloat16)
        grad_query = (
            jnp.einsum("hqk,khd->qhd", scores_low, keys_low, preferred_element_type=jnp.float32)
            * factor
        )
        grad_keys = (
            grad_keys
            + jnp.einsum("hqk,qhd->khd", scores_low, queries, preferred_element_type=jnp.float32)
            * factor
        )
        return ((grad_keys, grad_values), grad_query)

    zero_heads = jnp.zeros((seq_len, local_heads, HEAD_DIM), jnp.float32)
    (grad_keys, grad_values), grad_queries = lax.scan(
        attn_back, (zero_heads, zero_heads), jnp.arange(block_count, dtype=jnp.int32)
    )
    grad_queries = rotate_back(
        grad_queries.reshape(seq_len, local_heads, HEAD_DIM), cosine, sine_tab
    )
    grad_keys = rotate_back(grad_keys, cosine, sine_tab)
    grad_proj = (
        jnp.stack([grad_queries, grad_keys, grad_values], axis=0)
        .reshape(3, seq_len, local_width)
        .astype(jnp.bfloat16)
    )
    grad_bias_local = jnp.sum(grad_proj, axis=1, dtype=jnp.float32)
    grad_qkv = jnp.einsum(
        "sd,csh->cdh", normed_group, grad_proj, preferred_element_type=jnp.float32
    )
    normed_one_part = jnp.einsum(
        "csh,cdh->sd", grad_proj, full_qkv, preferred_element_type=jnp.float32
    )
    grad_normed_one = lax.psum_scatter(
        normed_one_part.astype(jnp.bfloat16), "shard", scatter_dimension=0, tiled=True
    ).astype(jnp.float32)
    grad_hidden_own = lax.dynamic_slice_in_dim(grad_hidden, first_own, own_rows, 0)
    grad_tokens = grad_hidden_own + norm_back(grad_normed_one, unit_one, scale_one, gain_attn)
    grad_gain_one = jnp.sum(grad_normed_one * unit_one, axis=0)
    grad_bias_full = lax.dynamic_update_slice_in_dim(
        jnp.zeros((3, model_width), jnp.float32), grad_bias_local, shard_pos * local_width, 1
    )
    qkv_grad_part, wout_grad_part, shared_grad_in, shared_grad_down = (
        lax.psum_scatter(
            grad_qkv.astype(jnp.bfloat16), "expert", scatter_dimension=1, tiled=True
        ).astype(jnp.float32),
        lax.psum_scatter(
            grad_wout.astype(jnp.bfloat16), "expert", scatter_dimension=1, tiled=True
        ).astype(jnp.float32),
        lax.psum_scatter(
            grad_sgu.astype(jnp.bfloat16), "expert", scatter_dimension=1, tiled=True
        ).astype(jnp.float32),
        lax.psum_scatter(
            grad_sdown.astype(jnp.bfloat16), "expert", scatter_dimension=1, tiled=True
        ).astype(jnp.float32),
    )
    router_total, gain_one_total, gain_two_total, gate_total, bias_total = lax.psum(
        (grad_router, grad_gain_one, grad_gain_two, grad_gate_vec, grad_bias_full),
        ("expert", "shard"),
    )
    return (
        result,
        grad_tokens,
        gain_one_total,
        qkv_grad_part,
        bias_total,
        wout_grad_part,
        gain_two_total,
        router_total,
        gate_total,
        shared_grad_in,
        shared_grad_down,
        grad_expert_gu[None],
        grad_expert_down[None],
    )


def solution(mesh):
    return jax.shard_map(
        local,
        mesh=mesh,
        in_specs=(
            P(("expert", "shard"), None),
            P(),
            P(None, "expert", "shard"),
            P(None, "shard"),
            P("shard", "expert"),
            P(),
            P(),
            P(),
            P(None, "expert", "shard"),
            P("shard", "expert"),
            P(("expert", "shard"), None, None, None),
            P(("expert", "shard"), None, None),
            P(("expert", "shard"), None),
            P(("expert", "shard"), None),
        ),
        out_specs=(
            P(("expert", "shard"), None),
            P(("expert", "shard"), None),
            P(),
            P(None, "expert", "shard"),
            P(),
            P("shard", "expert"),
            P(),
            P(),
            P(),
            P(None, "expert", "shard"),
            P("shard", "expert"),
            P(("expert", "shard"), None, None, None),
            P(("expert", "shard"), None, None),
        ),
        check_vma=False,
    )
```

profile of v0, /device:TPU:0, one launch (start us, length us, event | category | flops | bytes accessed | tf_op | source)
XLA Modules:
  0.0 1700.8 jit_solution(9462223077759114342)
XLA Ops:
  16.6 19.8 %all-gather.10.cloned.1.call-done = bf16[512,2048]{1,0:T(8,128)(2,1)} async-done(((bf16[128,2048]{1,0:T(8,128)(2,1)}), bf16[512,2048]{1,0:T(8,128)(2,1)}) %all-gather.10.cloned.1.call-update) | async-done | bytes 2097168 | tf_op jit(solution)/shard_map/all_gather | solution.py:113
  36.5 102.1 %all-gather.12.cloned.1.call-done = bf16[3,2048,512]{1,2,0:T(8,128)(2,1)} async-done(((bf16[3,256,512]{1,2,0:T(8,128)(2,1)}), bf16[3,2048,512]{1,2,0:T(8,128)(2,1)}) %all-gather.12.cloned.1.call-update) | async-done | bytes 6291472 | tf_op jit(solution)/shard_map/all_gather | solution.py:103
  150.0 39.2 %all-gather.14.cloned.1.call-done = bf16[512,2048]{1,0:T(8,128)(2,1)} async-done(((bf16[512,256]{1,0:T(8,128)(2,1)}), bf16[512,2048]{1,0:T(8,128)(2,1)}) %all-gather.14.cloned.1.call-update) | async-done | bytes 2097168 | tf_op jit(solution)/shard_map/all_gather | solution.py:104
  196.9 14.5 all-gather.8.cloned.1.call-done
  211.4 88.3 %all-reduce.5.cloned.1.call-done = f32[512,2048]{1,0:T(8,128)} async-done(((f32[512,2048]{1,0:T(8,128)}), f32[512,2048]{1,0:T(8,128)}) %all-reduce.5.cloned.1.call-update) | async-done | bytes 4194320 | tf_op jit(solution)/shard_map/psum | solution.py:140
  343.1 175.8 %all-to-all-done = bf16[32,32,2048]{2,1,0:T(8,128)(2,1)} async-done(((bf16[32,32,2048]{2,1,0:T(8,128)(2,1)}), bf16[32,32,2048]{2,1,0:T(8,128)(2,1)}, u32[]{:S(2)}, u32[]{:S(2)}) %all-to-all-start) | async-done | bytes 4194336 | tf_op jit(solution)/shard_map/all_to_all | solution.py:100
  524.0 18.6 %fusion.4 = f32[2,1024,1408]{2,1,0:T(8,128)} fusion(bf16[1024,2048,1]{1,0,2:T(8,128)(2,1)} %bitcast.18, bf16[1,2,2048,1408]{3,2,1,0:T(8,128)(2,1)} %param.24), kind=kOutput, calls=%fused_computation.13 | convolution fusion | flops 11811160064 | bytes 27262976 | tf_op jit(solution)/shard_map/rd,cdf->crf/dot_general | solution.py:176
  542.6 92.2 %all-to-all-done.2 = bf16[32,32,2048]{2,1,0:T(8,128)(2,1)} async-done(((bf16[32,32,2048]{2,1,0:T(8,128)(2,1)}), bf16[32,32,2048]{2,1,0:T(8,128)(2,1)}, u32[]{:S(2)}, u32[]{:S(2)}) %all-to-all-start.2) | async-done | bytes 4194336 | tf_op jit(solution)/shard_map/all_to_all | solution.py:100
  634.9 14.1 fusion.32
  649.0 18.4 %bitcast_convert_fusion = bf16[1024,2048]{1,0:T(8,128)(2,1)} fusion(bf16[1,2,2048,1408]{3,2,1,0:T(8,128)(2,1)} %param.24, bf16[1,1024,1408]{2,1,0:T(8,128)(2,1)S(1)} %get-tuple-element.125, bf16[1,1024,1408]{2,1,0:T(8,128)(2,1)S(1)} %get-tuple-element.124), kind=kOutput, calls=%fused_computation.11 | convolution fusion | flops 11816140800 | bytes 21495808 | tf_op jit(solution)/shard_map/crf,cdf->rd/dot_general | solution.py:210
  691.2 120.5 %all-to-all-done.3 = bf16[32,32,2048]{2,1,0:T(8,128)(2,1)} async-done(((bf16[32,32,2048]{2,1,0:T(8,128)(2,1)}), bf16[32,32,2048]{2,1,0:T(8,128)(2,1)}, u32[]{:S(2)}, u32[]{:S(2)}) %all-to-all-start.3) | async-done | bytes 4194336 | tf_op jit(solution)/shard_map/all_to_all | solution.py:100
  844.9 11.2 convolution_bitcast_fusion.3
  856.1 24.5 %reduce-scatter.7.cloned.1.call-done = bf16[128,2048]{1,0:T(8,128)(2,1)} async-done(((bf16[512,2048]{1,0:T(8,128)(2,1)}), bf16[128,2048]{1,0:T(8,128)(2,1)}) %reduce-scatter.7.cloned.1.call-update) | async-done | bytes 524304 | tf_op jit(solution)/shard_map/reduce_scatter | solution.py:152
  894.7 14.5 all-to-all-done.1
  946.1 76.5 %all-reduce.7.cloned.1.call-done = f32[512,2048]{1,0:T(8,128)} async-done(((f32[512,2048]{1,0:T(8,128)}), f32[512,2048]{1,0:T(8,128)}) %all-reduce.7.cloned.1.call-update) | async-done | bytes 4194320 | tf_op jit(solution)/shard_map/psum | solution.py:256
  1082.6 20.0 %convolution_bitcast_fusion = f32[1,2,2048,1408]{2,3,1,0:T(8,128)} fusion(bf16[1024,2048,1]{1,0,2:T(8,128)(2,1)} %bitcast.18, bf16[1,1024,1408]{2,1,0:T(8,128)(2,1)} %copy-done.53, bf16[1,1024,1408]{2,1,0:T(8,128)(2,1)} %copy-done.52), kind=kOutput, calls=%fused_computation.4 | convolution fusion | flops 11814043648 | bytes 33030144 | tf_op jit(solution)/shard_map/rd,crf->cdf/dot_general | solution.py:207
  1102.7 23.4 %copy.123 = f32[1,2,2048,1408]{3,2,1,0:T(8,128)} copy(f32[1,2,2048,1408]{2,3,1,0:T(8,128)} %convolution_bitcast_fusion) | data formatting | bytes 46137344
  1126.0 11.5 convolution_bitcast_fusion.1
  1145.6 24.9 %reduce-scatter.9.cloned.1.call-done = bf16[128,2048]{1,0:T(8,128)(2,1)} async-done(((bf16[512,2048]{1,0:T(8,128)(2,1)}), bf16[128,2048]{1,0:T(8,128)(2,1)}) %reduce-scatter.9.cloned.1.call-update) | async-done | bytes 524304 | tf_op jit(solution)/shard_map/reduce_scatter | solution.py:317
  1174.7 68.2 %reduce-scatter.13.cloned.1.call-done = bf16[512,256]{1,0:T(8,128)(2,1)} async-done(((bf16[512,2048]{1,0:T(8,128)(2,1)}), bf16[512,256]{1,0:T(8,128)(2,1)}) %reduce-scatter.13.cloned.1.call-update) | async-done | bytes 262160 | tf_op jit(solution)/shard_map/reduce_scatter | solution.py:330
  1244.7 43.5 %all-reduce = (f32[2048]{0:T(1024)}, f32[3,2048]{1,0:T(4,128)}, f32[2048]{0:T(1024)}, f32[2048]{0:T(1024)}) all-reduce(f32[2048]{0:T(1024)S(1)} %get-tuple-element.112, f32[3,2048]{1,0:T(4,128)S(1)} %constant_dynamic-update-slice_fusion, f32[2048]{0:T(1024)S(1)} %fusion.72, ...), channel_id=1, replica_groups=mesh['expert'=8,'shard'=4] {'expert','shard'}, use_global_device_ids=true, to_apply=%region_25.26 | all-reduce | flops 12288 | bytes 98304 | tf_op jit(solution)/shard_map/psum | solution.py:340
  1288.2 151.3 %reduce-scatter.15.cloned.1.call-done = bf16[2,256,1408]{1,2,0:T(8,128)(2,1)} async-done(((bf16[2,2048,1408]{1,2,0:T(8,128)(2,1)}), bf16[2,256,1408]{1,2,0:T(8,128)(2,1)}) %reduce-scatter.15.cloned.1.call-update) | async-done | bytes 1441808 | tf_op jit(solution)/shard_map/reduce_scatter | solution.py:333
  1442.4 118.1 %reduce-scatter.11.cloned.1.call-done = bf16[3,256,512]{1,2,0:T(8,128)(2,1)} async-done(((bf16[3,2048,512]{1,2,0:T(8,128)(2,1)}), bf16[3,256,512]{1,2,0:T(8,128)(2,1)}) %reduce-scatter.11.cloned.1.call-update) | async-done | bytes 786448 | tf_op jit(solution)/shard_map/reduce_scatter | solution.py:327
  1563.1 129.2 %all-reduce.9.cloned.1.call-done = f32[2048,32]{0,1:T(8,128)} async-done(((f32[2048,32]{0,1:T(8,128)}), f32[2048,32]{0,1:T(8,128)}) %all-reduce.9.cloned.1.call-update) | async-done | bytes 262160 | tf_op jit(solution)/shard_map/psum | solution.py:340
  (251 shorter events, 265.5 us)
Async XLA Ops:
  7.2 326.7 %copy-start = (bf16[2048,32]{0,1:T(8,128)(2,1)S(1)}, bf16[2048,32]{0,1:T(8,128)(2,1)}, u32[]{:S(2)}) copy-start(bf16[2048,32]{0,1:T(8,128)(2,1)} %param.20) | copy-start | bytes 393220
  7.2 131.4 %copy-start.50 = (f32[3,512]{1,0:T(4,128)S(1)}, f32[3,512]{1,0:T(4,128)}, u32[]{:S(2)}) copy-start(f32[3,512]{1,0:T(4,128)} %param.17) | copy-start | bytes 18436
  7.2 29.3 %all-gather.10.cloned.1.call-start = ((), (), s32[]{:S(2)}) async-start(), calls=%async_computation.11 | async-start | bytes 2621440 | tf_op jit(solution)/shard_map/all_gather | solution.py:113
  11.0 127.6 %all-gather.12.cloned.1.call-start = ((), (), s32[]{:S(2)}) async-start(), calls=%async_computation.12 | async-start | bytes 7077888 | tf_op jit(solution)/shard_map/all_gather | solution.py:103
  13.4 175.8 %all-gather.14.cloned.1.call-start = ((), (), s32[]{:S(2)}) async-start(), calls=%async_computation.13 | async-start | bytes 2359296 | tf_op jit(solution)/shard_map/all_gather | solution.py:104
  14.1 197.3 %all-gather.8.cloned.1.call-start = ((), (), s32[]{:S(2)}) async-start(), calls=%async_computation.10 | async-start | bytes 2621440 | tf_op jit(solution)/shard_map/all_gather | solution.py:112
  14.7 285.0 %all-reduce.5.cloned.1.call-start = ((), (), s32[]{:S(2)}) async-start(), calls=%async_computation.14 | async-start | bytes 8388608 | tf_op jit(solution)/shard_map/psum | solution.py:140
  194.1 621.4 %all-gather.16.cloned.1.call-start = ((), (), s32[]{:S(2)}) async-start(), calls=%async_computation.15 | async-start | bytes 12976128 | tf_op jit(solution)/shard_map/all_gather | solution.py:105
  196.9 106.3 %copy-start.36 = (f32[2048]{0:T(1024)S(1)}, f32[2048]{0:T(1024)}, u32[]{:S(2)}) copy-start(f32[2048]{0:T(1024)} %param.19) | copy-start | bytes 24580
  320.2 198.6 %all-to-all-start = ((bf16[32,32,2048]{2,1,0:T(8,128)(2,1)}), bf16[32,32,2048]{2,1,0:T(8,128)(2,1)}, u32[]{:S(2)}, u32[]{:S(2)}) async-start(bf16[32,32,2048]{2,1,0:T(8,128)(2,1)} %bitcast.208), calls=%async_computation.1 | async-start | bytes 8388608 | tf_op jit(solution)/shard_map/all_to_all | solution.py:100
  518.9 116.0 %all-to-all-start.2 = ((bf16[32,32,2048]{2,1,0:T(8,128)(2,1)}), bf16[32,32,2048]{2,1,0:T(8,128)(2,1)}, u32[]{:S(2)}, u32[]{:S(2)}) async-start(bf16[32,32,2048]{2,1,0:T(8,128)(2,1)} %bitcast.207), calls=%async_computation.3 | async-start | bytes 8388608 | tf_op jit(solution)/shard_map/all_to_all | solution.py:100
  522.5 304.1 %all-gather.20.cloned.1.call-start = ((), (), s32[]{:S(2)}) async-start(), calls=%async_computation.18 | async-start | bytes 2621440 | tf_op jit(solution)/shard_map/all_gather | solution.py:240
  523.2 303.4 %all-gather.18.cloned.1.call-start = ((), (), s32[]{:S(2)}) async-start(), calls=%async_computation.16 | async-start | bytes 6488064 | tf_op jit(solution)/shard_map/all_gather | solution.py:106
  667.4 144.2 %all-to-all-start.3 = ((bf16[32,32,2048]{2,1,0:T(8,128)(2,1)}), bf16[32,32,2048]{2,1,0:T(8,128)(2,1)}, u32[]{:S(2)}, u32[]{:S(2)}) async-start(bf16[32,32,2048]{2,1,0:T(8,128)(2,1)} %bitcast.214), calls=%async_computation.4 | async-start | bytes 8388608 | tf_op jit(solution)/shard_map/all_to_all | solution.py:100
  811.6 97.5 %all-to-all-start.1 = ((bf16[32,32,2048]{2,1,0:T(8,128)(2,1)}), bf16[32,32,2048]{2,1,0:T(8,128)(2,1)}, u32[]{:S(2)}, u32[]{:S(2)}) async-start(bf16[32,32,2048]{2,1,0:T(8,128)(2,1)} %bitcast.213), calls=%async_computation.2 | async-start | bytes 8388608 | tf_op jit(solution)/shard_map/all_to_all | solution.py:100
  815.5 65.2 %reduce-scatter.7.cloned.1.call-start = ((), (), s32[]{:S(2)}) async-start(), calls=%async_computation.17 | async-start | bytes 2621440 | tf_op jit(solution)/shard_map/reduce_scatter | solution.py:152
  843.4 179.2 %all-reduce.7.cloned.1.call-start = ((), (), s32[]{:S(2)}) async-start(), calls=%async_computation.19 | async-start | bytes 8388608 | tf_op jit(solution)/shard_map/psum | solution.py:256
  937.5 205.7 %reduce-scatter.17.cloned.1.call-start = ((), (), s32[]{:S(2)}) async-start(), calls=%async_computation.25 | async-start | bytes 6488064 | tf_op jit(solution)/shard_map/reduce_scatter | solution.py:336
  945.4 77.2 %copy-start.37 = (f32[2048]{0:T(1024)S(1)}, f32[2048]{0:T(1024)}, u32[]{:S(2)}) copy-start(f32[2048]{0:T(1024)} %param.19) | copy-start | bytes 24580
  945.5 225.0 %reduce-scatter.9.cloned.1.call-start = ((), (), s32[]{:S(2)}) async-start(), calls=%async_computation.20 | async-start | bytes 2621440 | tf_op jit(solution)/shard_map/reduce_scatter | solution.py:317
  1058.3 184.6 %reduce-scatter.13.cloned.1.call-start = ((), (), s32[]{:S(2)}) async-start(), calls=%async_computation.22 | async-start | bytes 2359296 | tf_op jit(solution)/shard_map/reduce_scatter | solution.py:330
  1063.5 376.0 %reduce-scatter.15.cloned.1.call-start = ((), (), s32[]{:S(2)}) async-start(), calls=%async_computation.24 | async-start | bytes 12976128 | tf_op jit(solution)/shard_map/reduce_scatter | solution.py:333
  1074.5 486.0 %reduce-scatter.11.cloned.1.call-start = ((), (), s32[]{:S(2)}) async-start(), calls=%async_computation.21 | async-start | bytes 7077888 | tf_op jit(solution)/shard_map/reduce_scatter | solution.py:327
  1082.6 609.6 %all-reduce.9.cloned.1.call-start = ((), (), s32[]{:S(2)}) async-start(), calls=%async_computation.23 | async-start | bytes 524288 | tf_op jit(solution)/shard_map/psum | solution.py:340
  (50 other events, 401.6 us)
Sparse Core Ops, SparseCore 0:
  11.1 25.2 all-gather.9
  39.1 99.4 all-gather.11
  140.6 48.5 all-gather.13
  190.6 20.7 all-gather.7
  214.2 85.4 all-reduce.4
  301.8 304.9 all-gather.15
  608.3 26.5 all-gather.19
  636.9 156.9 all-gather.17
  843.5 37.0 reduce-scatter.6
  937.7 84.9 all-reduce.6
  1026.3 111.1 reduce-scatter.16
  1139.9 30.5 reduce-scatter.8
  1174.0 68.8 reduce-scatter.12
  1246.4 193.0 reduce-scatter.14
  1442.9 117.5 reduce-scatter.10
  1566.4 125.7 all-reduce.8
where the time goes:
time: 1710 us; the launch traced here: 1700 us
  waiting for transfers between devices  1260 us (74%)
  matrix products  197 us (12%)
  local copies, waits for them, and re-layouts  99.1 us (6%)
  other arithmetic  65.1 us (4%)
  blocking collectives  43.5 us (3%)
  starting transfers between devices  19.1 us (1%)
    all_to_all x4, waiting for transfers between devices, route_rows(): lax.all_to_all(block, ('expert', 'shard'), split_axis=0, concat_axis=0, t...  403 us
    reduce_scatter x1, waiting for transfers between devices, local(): lax.psum_scatter(grad_sgu.astype(jnp.bfloat16), 'expert', scatter_dimensi...  151 us
    psum x1, waiting for transfers between devices, local(): lax.psum((grad_router, grad_gain_one, grad_gain_two, grad_gate_vec, grad_...  129 us
    reduce_scatter x1, waiting for transfers between devices, local(): lax.psum_scatter(grad_qkv.astype(jnp.bfloat16), 'expert', scatter_dimensi...  118 us
    all_gather x1, waiting for transfers between devices, local(): lax.all_gather(w_qkv, 'expert', axis=1, tiled=True)  102 us
    psum x1, waiting for transfers between devices, local(): attn_group = lax.psum(attn_part, 'shard')  88.3 us
    psum x1, waiting for transfers between devices, local(): grad_normed_two = lax.psum(normed_part, 'shard')  76.5 us
    reduce_scatter x1, waiting for transfers between devices, local(): lax.psum_scatter(grad_wout.astype(jnp.bfloat16), 'expert', scatter_dimens...  68.2 us
  transfers between devices with their start and end apart: 20, of which 16 were waited for; matrix products, arithmetic and copies ran while one was open for 19% of the time, Pallas kernels for 0%

commit v1 on v0

v1 whole, which is shorter than its diff:
```python
import functools

import jax
import jax.numpy as jnp
from jax import lax
from jax.experimental import pallas as pl
from jax.experimental.pallas import tpu as pltpu
from jax.sharding import PartitionSpec as P

HEAD_DIM = 128
TOPK = 4
EXPERT = "expert"
SHARD = "shard"
both = (EXPERT, SHARD)
eps = 1e-06
rope_base = 1000000.0
highest = lax.Precision.HIGHEST

MESH_ID = pl.DeviceIdType.MESH


class Place:
    def __init__(self, levels):
        self.levels = levels
        spot, lane = lax.axis_index(EXPERT), lax.axis_index(SHARD)
        self.z, self.y = spot // 2, spot % 2
        self.x, self.c = lane // 2, lane % 2

    def device(self, z=None, y=None, x=None, c=None):
        z = self.z if z is None else z
        y = self.y if y is None else y
        x = self.x if x is None else x
        c = self.c if c is None else c
        return {EXPERT: z * 2 + y, SHARD: x * 2 + c}

    def flat(self, z, y, x, c):
        return ((z * 2 + y) * 2 + x) * 2 + c


def greet(place, targets, ends):
    barrier = pltpu.get_barrier_semaphore()
    for target in targets:
        pl.semaphore_signal(barrier, inc=1, device_id=target, device_id_type=MESH_ID)
    count = len(targets)
    if ends:
        @pl.when(place.z > 0)
        def _():
            pl.semaphore_signal(
                barrier, inc=1, device_id=place.device(z=place.z - 1), device_id_type=MESH_ID
            )

        @pl.when(place.z < place.levels - 1)
        def _():
            pl.semaphore_signal(
                barrier, inc=1, device_id=place.device(z=place.z + 1), device_id_type=MESH_ID
            )

        inner = (place.z > 0).astype(jnp.int32) + (place.z < place.levels - 1).astype(jnp.int32)
        count = count + inner
    pl.semaphore_wait(barrier, count)


def gather_steps(levels, sources, outs, own_sem, send_sems, recv_sems):
    place = Place(levels)
    z, y, x, c = place.z, place.y, place.x, place.c
    top = levels - 1
    x_dev, y_dev, c_dev = place.device(x=1 - x), place.device(y=1 - y), place.device(c=1 - c)

    class Copies:
        def __init__(self, kind, level, refs_from, refs_to, device):
            self.each = [
                pltpu.make_async_remote_copy(
                    src_ref=ref,
                    dst_ref=dst,
                    send_sem=send_sems.at[kind, level, i],
                    recv_sem=recv_sems.at[kind, level, i],
                    device_id=device,
                    device_id_type=MESH_ID,
                )
                for i, (ref, dst) in enumerate(zip(refs_from, refs_to))
            ]

        def start(self):
            for one in self.each:
                one.start()

        def wait_recv(self):
            for one in self.each:
                one.wait_recv()

        def wait_send(self):
            for one in self.each:
                one.wait_send()

    copy = Copies

    def block(level, yy, xx, cc):
        return [out.at[place.flat(level, yy, xx, cc)] for out in outs]

    def part(level, yy, xx, cc, side):
        flat = place.flat(level, yy, xx, cc)
        return [
            out.at[flat, pl.ds(side * (out.shape[1] // 2), out.shape[1] // 2)] for out in outs
        ]

    UP, DOWN, XN, YN, DX, DY, CO, CX, CY, CDX, CDY = range(11)

    def dst_of(kind, level):
        if kind in (UP, DOWN):
            return block(level, y, x, c)
        if kind == XN:
            return block(level, y, 1 - x, c)
        if kind == YN:
            return block(level, 1 - y, x, c)
        if kind == DX:
            return part(level, 1 - y, 1 - x, c, 0)
        if kind == DY:
            return part(level, 1 - y, 1 - x, c, 1)
        if kind == CO:
            return block(level, y, x, 1 - c)
        if kind == CX:
            return block(level, y, 1 - x, 1 - c)
        if kind == CY:
            return block(level, 1 - y, x, 1 - c)
        if kind == CDX:
            return part(level, 1 - y, 1 - x, 1 - c, 0)
        return part(level, 1 - y, 1 - x, 1 - c, 1)

    def arrived(kind, level):
        ref = dst_of(kind, level)
        copy(kind, level, ref, ref, c_dev).wait_recv()

    def sent(kind, level, ref):
        copy(kind, level, ref, ref, c_dev).wait_send()

    def spread(level, ref):
        copy(XN, level, ref, block(level, y, x, c), x_dev).start()
        copy(YN, level, ref, block(level, y, x, c), y_dev).start()
        copy(CO, level, ref, block(level, y, x, c), c_dev).start()

    def at_distance(t, action):
        if t == 0:
            action(z)
            return

        @pl.when(z - t >= 0)
        def _():
            action(z - t)

        @pl.when(z + t <= top)
        def _():
            action(z + t)

    def from_neighbours(level):
        arrived(XN, level)
        ref = part(level, y, 1 - x, c, 1)
        copy(DY, level, ref, ref, y_dev).start()
        ref = block(level, y, 1 - x, c)
        copy(CX, level, ref, ref, c_dev).start()
        arrived(YN, level)
        ref = part(level, 1 - y, x, c, 0)
        copy(DX, level, ref, ref, x_dev).start()
        ref = block(level, 1 - y, x, c)
        copy(CY, level, ref, ref, c_dev).start()

    def from_diagonal(level):
        arrived(DX, level)
        ref = part(level, 1 - y, 1 - x, c, 0)
        copy(CDX, level, ref, ref, c_dev).start()
        arrived(DY, level)
        ref = part(level, 1 - y, 1 - x, c, 1)
        copy(CDY, level, ref, ref, c_dev).start()

    def start():
        greet(place, [x_dev, y_dev, c_dev], True)
        for i, (ref, dst) in enumerate(zip(sources, block(z, y, x, c))):
            pltpu.make_async_copy(ref, dst, own_sem.at[i]).start()

        @pl.when(z < top)
        def _():
            copy(UP, z, sources, block(z, y, x, c), place.device(z=z + 1)).start()

        @pl.when(z > 0)
        def _():
            copy(DOWN, z, sources, block(z, y, x, c), place.device(z=z - 1)).start()

        spread(z, sources)

    def onward(t):
        if t < levels:
            @pl.when(z - t >= 0)
            def _():
                level = z - t
                arrived(UP, level)
                ref = block(level, y, x, c)

                @pl.when(z < top)
                def _():
                    copy(UP, level, ref, ref, place.device(z=z + 1)).start()

                spread(level, ref)

            @pl.when(z + t <= top)
            def _():
                level = z + t
                arrived(DOWN, level)
                ref = block(level, y, x, c)

                @pl.when(z > 0)
                def _():
                    copy(DOWN, level, ref, ref, place.device(z=z - 1)).start()

                spread(level, ref)

        if t - 1 < levels:
            at_distance(t - 1, from_neighbours)
        if 0 <= t - 2 < levels:
            at_distance(t - 2, from_diagonal)


    def finish():
        for i, (ref, dst) in enumerate(zip(sources, block(z, y, x, c))):
            pltpu.make_async_copy(ref, dst, own_sem.at[i]).wait()
        for level in range(levels):
            for kind in (CO, CX, CY, CDX, CDY):
                arrived(kind, level)
            for kind in (XN, YN, DX, DY, CO, CX, CY, CDX, CDY):
                sent(kind, level, dst_of(kind, level))

            @pl.when((z < top) & (level <= z))
            def _():
                sent(UP, level, dst_of(UP, level))

            @pl.when((z > 0) & (level >= z))
            def _():
                sent(DOWN, level, dst_of(DOWN, level))

    middle = [functools.partial(onward, t) for t in range(1, levels + 2)]
    return [start] + middle + [finish]


def gather_kernel(levels, size, *refs):
    sources, outs = refs[:size], refs[size : 2 * size]
    for step in gather_steps(levels, sources, outs, *refs[2 * size :]):
        step()


def gather_all(arrays, levels, count, ident):
    size = len(arrays)
    outs = pl.pallas_call(
        functools.partial(gather_kernel, levels, size),
        out_shape=[jax.ShapeDtypeStruct((count,) + a.shape, a.dtype) for a in arrays],
        in_specs=[pl.BlockSpec(memory_space=pltpu.VMEM)] * size,
        out_specs=[pl.BlockSpec(memory_space=pl.ANY)] * size,
        scratch_shapes=[
            pltpu.SemaphoreType.DMA((size,)),
            pltpu.SemaphoreType.DMA((11, levels, size)),
            pltpu.SemaphoreType.DMA((11, levels, size)),
        ],
        compiler_params=pltpu.CompilerParams(collective_id=ident, has_side_effects=True),
        name="gather_all",
    )(*arrays)
    return [out.reshape((-1,) + out.shape[2:]) for out in outs]


def scatter_steps(
    levels, part, out, from_c, from_d, from_xy, from_z, load, load_sem, send_sem, recv_sem
):
    place = Place(levels)
    z, y, x, c = place.z, place.y, place.x, place.c
    top = levels - 1
    width = part.shape[-1]
    half = width // 2
    x_dev, y_dev, c_dev = place.device(x=1 - x), place.device(y=1 - y), place.device(c=1 - c)
    OWN, XN, YN, DIAG = 0, 1, 2, 3
    CORE, TOX, TOY, DX, DY, UP, DOWN = 0, 4, 5, 6, 7, 8, 9

    def columns(col):
        return {OWN: (y, x), XN: (y, 1 - x), YN: (1 - y, x), DIAG: (1 - y, 1 - x)}[col]

    def copy(kind, level, ref, dst, device):
        return pltpu.make_async_remote_copy(
            src_ref=ref,
            dst_ref=dst,
            send_sem=send_sem.at[kind, level],
            recv_sem=recv_sem.at[kind, level],
            device_id=device,
            device_id_type=MESH_ID,
        )

    def block(level, col, cc):
        yy, xx = columns(col)
        return part.at[place.flat(level, yy, xx, cc)]

    def core_copy(level, col):
        return copy(CORE + col, level, block(level, col, 1 - c), from_c.at[col, level], c_dev)

    def load_copy(level, col):
        return pltpu.make_async_copy(block(level, col, c), load.at[col, level], load_sem.at[col, level])

    def at_distance(t, action):
        if t == 0:
            action(z)
            return

        @pl.when(z - t >= 0)
        def _():
            action(z - t)

        @pl.when(z + t <= top)
        def _():
            action(z + t)

    def each_level(action):
        for t in range(levels - 1, -1, -1):
            at_distance(t, action)

    def start():
        greet(place, [x_dev, y_dev, c_dev], True)
        for col in (DIAG, XN, YN, OWN):
            def begin(level):
                core_copy(level, col).start()
                load_copy(level, col).start()
            each_level(begin)

    def strips(action):
        def step(i, carry):
            action(pl.ds(pl.multiple_of(i * 16, 16), 16))
            return carry
        lax.fori_loop(0, part.shape[1] // 16, step, 0)

    def f32(ref, *where):
        return ref[where].astype(jnp.float32)

    low, high = slice(0, half), slice(half, width)

    def diagonal(level):
        load_copy(level, DIAG).wait()
        core_copy(level, DIAG).wait_recv()

        def add(rows):
            load[DIAG, level, rows] = (
                f32(load, DIAG, level, rows) + f32(from_c, DIAG, level, rows)
            ).astype(load.dtype)
        strips(add)
        copy(DX, level, load.at[DIAG, level, :, low], from_d.at[0, level], x_dev).start()
        copy(DY, level, load.at[DIAG, level, :, high], from_d.at[1, level], y_dev).start()

    def sides(level):
        for col, kind, side, goes, device in ((XN, DY, 1, TOX, x_dev), (YN, DX, 0, TOY, y_dev)):
            load_copy(level, col).wait()
            core_copy(level, col).wait_recv()
            copy(kind, level, from_d.at[side, level], from_d.at[side, level], device).wait_recv()
            mine, other = (high, low) if side else (low, high)

            def add(rows):
                load[col, level, rows, mine] = (
                    f32(load, col, level, rows, mine)
                    + f32(from_c, col, level, rows, mine)
                    + f32(from_d, side, level, rows)
                ).astype(load.dtype)
                load[col, level, rows, other] = (
                    f32(load, col, level, rows, other) + f32(from_c, col, level, rows, other)
                ).astype(load.dtype)
            strips(add)
            copy(goes, level, load.at[col, level], from_xy.at[goes - TOX, level], device).start()

    def await_column(level):
        load_copy(level, OWN).wait()
        core_copy(level, OWN).wait_recv()
        copy(TOX, level, from_xy.at[0, level], from_xy.at[0, level], x_dev).wait_recv()
        copy(TOY, level, from_xy.at[1, level], from_xy.at[1, level], y_dev).wait_recv()

    def column(level, rows):
        return (
            f32(load, OWN, level, rows)
            + f32(from_c, OWN, level, rows)
            + f32(from_xy, 0, level, rows)
            + f32(from_xy, 1, level, rows)
        )


    def pass_on(level, kind, first, target, slot):
        await_column(level)

        @pl.when(first)
        def _():
            def add(rows):
                load[OWN, level, rows] = column(level, rows).astype(load.dtype)
            strips(add)

        @pl.when(jnp.logical_not(first))
        def _():
            copy(kind, level, from_z.at[level], from_z.at[level], c_dev).wait_recv()

            def add(rows):
                load[OWN, level, rows] = (
                    column(level, rows) + f32(from_z, level, rows)
                ).astype(load.dtype)
            strips(add)
        copy(kind, level, load.at[OWN, level], from_z.at[slot], target).start()

    def along_z(t):
        @pl.when(z + t <= top)
        def _():
            pass_on(z + t, UP, z == 0, place.device(z=z + 1), z + t)

        @pl.when(z - t >= 0)
        def _():
            slot = (z - t) if t > 1 else levels
            pass_on(z - t, DOWN, z == top, place.device(z=z - 1), slot)

    def finish_all():
        await_column(z)

        def add(rows):
            out[rows] = column(z, rows)
        strips(add)

        @pl.when(z > 0)
        def _():
            copy(UP, z, from_z.at[z], from_z.at[z], c_dev).wait_recv()

            def add(rows):
                out[rows] += f32(from_z, z, rows)
            strips(add)

        @pl.when(z < top)
        def _():
            copy(DOWN, z, from_z.at[levels], from_z.at[levels], c_dev).wait_recv()

            def add(rows):
                out[rows] += f32(from_z, levels, rows)
            strips(add)

        def finish(level):
            for col in (OWN, XN, YN, DIAG):
                core_copy(level, col).wait_send()
            copy(DX, level, from_d.at[0, level], from_d.at[0, level], x_dev).wait_send()
            copy(DY, level, from_d.at[1, level], from_d.at[1, level], y_dev).wait_send()
            copy(TOX, level, load.at[XN, level], from_xy.at[0, level], x_dev).wait_send()
            copy(TOY, level, load.at[YN, level], from_xy.at[1, level], y_dev).wait_send()

        for level in range(levels):
            finish(level)

            @pl.when(level > z)
            def _():
                copy(UP, level, load.at[OWN, level], from_z.at[level], c_dev).wait_send()

            @pl.when(level < z)
            def _():
                copy(DOWN, level, load.at[OWN, level], from_z.at[level], c_dev).wait_send()

    far = range(levels - 1, -1, -1)
    return (
        [start, functools.partial(each_level, diagonal)]
        + [functools.partial(at_distance, t, sides) for t in far]
        + [functools.partial(along_z, t) for t in far if t > 0]
        + [finish_all]
    )


def scatter_kernel(levels, *refs):
    for step in scatter_steps(levels, *refs):
        step()


def scatter_scratch(levels, rows, width, low):
    return [
        pltpu.VMEM((4, levels, rows, width), low),
        pltpu.VMEM((2, levels, rows, width // 2), low),
        pltpu.VMEM((2, levels, rows, width), low),
        pltpu.VMEM((levels + 1, rows, width), low),
        pltpu.VMEM((4, levels, rows, width), low),
        pltpu.SemaphoreType.DMA((4, levels)),
        pltpu.SemaphoreType.DMA((10, levels)),
        pltpu.SemaphoreType.DMA((10, levels)),
    ]


def scatter_all(part, levels, ident):
    count, rows, width = part.shape
    return pl.pallas_call(
        functools.partial(scatter_kernel, levels),
        out_shape=jax.ShapeDtypeStruct((rows, width), jnp.float32),
        in_specs=[pl.BlockSpec(memory_space=pl.ANY)],
        out_specs=pl.BlockSpec(memory_space=pltpu.VMEM),
        scratch_shapes=scatter_scratch(levels, rows, width, part.dtype),
        compiler_params=pltpu.CompilerParams(
            collective_id=ident, has_side_effects=True, vmem_limit_bytes=56 * 2**20
        ),
        name="scatter_all",
    )(part)


def lane_block(ref, index, width):
    return ref.at[:, pl.ds(pl.multiple_of(index * width, width), width)]


def gather_first_kernel(
    levels, qkv, wout, rows, qkv_all, wout_all, rows_all, own_sem, send_sem, recv_sem
):
    place = Place(levels)
    z, y, x, c = place.z, place.y, place.x, place.c
    top = levels - 1
    x_dev, y_dev, c_dev = place.device(x=1 - x), place.device(y=1 - y), place.device(c=1 - c)
    UP, DOWN, YN = range(3)
    pieces = 4
    row_kind = pieces * 3
    own_weights = [qkv.at[k] for k in range(3)] + [wout]

    def weight_refs(level, yy):
        spot = level * 2 + yy
        return [qkv_all.at[k, spot] for k in range(3)] + [
            lane_block(wout_all, spot, wout.shape[1])
        ]

    def copy(index, level, ref, dst, device):
        return pltpu.make_async_remote_copy(
            src_ref=ref,
            dst_ref=dst,
            send_sem=send_sem.at[index, level],
            recv_sem=recv_sem.at[index, level],
            device_id=device,
            device_id_type=MESH_ID,
        )

    def send(kind, level, refs, device, only=None):
        for i, (ref, dst) in enumerate(zip(refs, weight_refs(level, y))):
            if only in (None, i):
                copy(kind * pieces + i, level, ref, dst, device).start()

    def arrived(kind, level, only=None):
        for i, ref in enumerate(weight_refs(level, 1 - y if kind == YN else y)):
            if only in (None, i):
                copy(kind * pieces + i, level, ref, ref, c_dev).wait_recv()

    def sent(kind, level):
        for i, ref in enumerate(weight_refs(level, y)):
            copy(kind * pieces + i, level, ref, ref, c_dev).wait_send()

    greet(place, [x_dev, y_dev, c_dev], True)

    @pl.when(z < top)
    def _():
        send(UP, z, own_weights, place.device(z=z + 1))

    @pl.when(z > 0)
    def _():
        send(DOWN, z, own_weights, place.device(z=z - 1))

    send(YN, z, own_weights, y_dev)

    def row_ref(xx, cc):
        return rows_all.at[xx * 2 + cc]

    to_x = copy(row_kind, 0, rows, row_ref(x, c), x_dev)
    to_c = copy(row_kind, 1, rows, row_ref(x, c), c_dev)
    to_x.start()
    to_c.start()
    own = [
        pltpu.make_async_copy(ref, dst, own_sem.at[i])
        for i, (ref, dst) in enumerate(
            zip(own_weights + [rows], weight_refs(z, y) + [row_ref(x, c)])
        )
    ]
    for one in own:
        one.start()
    copy(row_kind, 0, rows, row_ref(1 - x, c), x_dev).wait_recv()
    on = copy(row_kind, 2, row_ref(1 - x, c), row_ref(1 - x, c), c_dev)
    on.start()

    def relay(kind, level, inner, target):
        for i in range(pieces):
            arrived(kind, level, i)

            @pl.when(inner)
            def _():
                send(kind, level, weight_refs(level, y), target, i)

            send(YN, level, weight_refs(level, y), y_dev, i)

    for t in range(1, levels):
        @pl.when(z - t >= 0)
        def _():
            relay(UP, z - t, z < top, place.device(z=z + 1))

        @pl.when(z + t <= top)
        def _():
            relay(DOWN, z + t, z > 0, place.device(z=z - 1))

    for one in own:
        one.wait()
    to_c.wait_recv()
    on.wait_recv()
    for one in (to_x, to_c, on):
        one.wait_send()
    for level in range(levels):
        arrived(YN, level)
        sent(YN, level)

        @pl.when((z < top) & (level <= z))
        def _():
            sent(UP, level)

        @pl.when((z > 0) & (level >= z))
        def _():
            sent(DOWN, level)


def gather_first(w_qkv, w_out, rows, levels, lanes, ident):
    spots = levels * 2
    qkv_all, wout_all, rows_all = pl.pallas_call(
        functools.partial(gather_first_kernel, levels),
        out_shape=[
            jax.ShapeDtypeStruct((3, spots) + w_qkv.shape[1:], w_qkv.dtype),
            jax.ShapeDtypeStruct((w_out.shape[0], spots * w_out.shape[1]), w_out.dtype),
            jax.ShapeDtypeStruct((lanes,) + rows.shape, rows.dtype),
        ],
        in_specs=[pl.BlockSpec(memory_space=pltpu.VMEM)] * 3,
        out_specs=[pl.BlockSpec(memory_space=pl.ANY)] * 3,
        scratch_shapes=[
            pltpu.SemaphoreType.DMA((5,)),
            pltpu.SemaphoreType.DMA((13, levels)),
            pltpu.SemaphoreType.DMA((13, levels)),
        ],
        compiler_params=pltpu.CompilerParams(collective_id=ident, has_side_effects=True),
        name="gather_first",
    )(w_qkv, w_out, rows)
    return (
        qkv_all.reshape(3, -1, w_qkv.shape[2]),
        wout_all,
        rows_all.reshape(-1, rows.shape[1]),
    )


def gather_lanes_kernel(levels, rows, rows_all, own_sem, send_sem, recv_sem):
    place = Place(levels)
    x, c = place.x, place.c
    x_dev, c_dev = place.device(x=1 - x), place.device(c=1 - c)

    def row_ref(xx, cc):
        return rows_all.at[xx * 2 + cc]

    def copy(index, ref, dst, device):
        return pltpu.make_async_remote_copy(
            src_ref=ref,
            dst_ref=dst,
            send_sem=send_sem.at[index],
            recv_sem=recv_sem.at[index],
            device_id=device,
            device_id_type=MESH_ID,
        )

    greet(place, [x_dev, c_dev], False)
    half = rows.shape[0] // 2
    parts = [pl.ds(0, half), pl.ds(half, half)]
    to_x = [copy(i, rows.at[p], row_ref(x, c).at[p], x_dev) for i, p in enumerate(parts)]
    to_c = copy(2, rows, row_ref(x, c), c_dev)
    own = pltpu.make_async_copy(rows, row_ref(x, c), own_sem)
    for one in to_x:
        one.start()
    to_c.start()
    own.start()
    on = []
    for i, p in enumerate(parts):
        to_x[i].wait_recv()
        on.append(copy(3 + i, row_ref(1 - x, c).at[p], row_ref(1 - x, c).at[p], c_dev))
        on[i].start()
    own.wait()
    to_c.wait()
    for one in on:
        one.wait()
    for one in to_x:
        one.wait_send()


def gather_lanes(rows, levels, lanes, ident):
    out = pl.pallas_call(
        functools.partial(gather_lanes_kernel, levels),
        out_shape=jax.ShapeDtypeStruct((lanes,) + rows.shape, rows.dtype),
        in_specs=[pl.BlockSpec(memory_space=pltpu.VMEM)],
        out_specs=pl.BlockSpec(memory_space=pltpu.VMEM),
        scratch_shapes=[
            pltpu.SemaphoreType.DMA,
            pltpu.SemaphoreType.DMA((5,)),
            pltpu.SemaphoreType.DMA((5,)),
        ],
        compiler_params=pltpu.CompilerParams(collective_id=ident, has_side_effects=True),
        name="gather_lanes",
    )(rows)
    return out.reshape(-1, rows.shape[1])


def scatter_lanes_kernel(levels, part, out, from_c, tx, from_x, send_sem, recv_sem):
    place = Place(levels)
    x, c = place.x, place.c
    x_dev, c_dev = place.device(x=1 - x), place.device(c=1 - c)
    rows = part.shape[1]
    pieces = 2
    size = rows // pieces

    def copy(index, ref, dst, device):
        return pltpu.make_async_remote_copy(
            src_ref=ref,
            dst_ref=dst,
            send_sem=send_sem.at[index],
            recv_sem=recv_sem.at[index],
            device_id=device,
            device_id_type=MESH_ID,
        )

    def strips(piece, action):
        def step(i, carry):
            action(pl.ds(pl.multiple_of(piece * size + i * 16, 16), 16))
            return carry
        lax.fori_loop(0, size // 16, step, 0)

    greet(place, [x_dev, c_dev], False)
    spans = [pl.ds(i * size, size) for i in range(pieces)]
    far = [
        copy(i, part.at[(1 - x) * 2 + 1 - c, p], from_c.at[0, p], c_dev)
        for i, p in enumerate(spans)
    ]
    near = copy(pieces, part.at[x * 2 + 1 - c], from_c.at[1], c_dev)
    for one in far:
        one.start()
    near.start()
    to_x = []
    for i, p in enumerate(spans):
        far[i].wait_recv()

        def add(span):
            tx[span] = (
                part[(1 - x) * 2 + c, span].astype(jnp.float32)
                + from_c[0, span].astype(jnp.float32)
            ).astype(tx.dtype)
        strips(i, add)
        to_x.append(copy(pieces + 1 + i, tx.at[p], from_x.at[p], x_dev))
        to_x[i].start()
    near.wait_recv()
    for i in range(pieces):
        to_x[i].wait_recv()

        def add(span):
            out[span] = (
                part[x * 2 + c, span].astype(jnp.float32)
                + from_c[1, span].astype(jnp.float32)
                + from_x[span].astype(jnp.float32)
            )
        strips(i, add)
    for one in far + [near] + to_x:
        one.wait_send()


def scatter_lanes(part, levels, lanes, ident):
    width = part.shape[1]
    rows = part.shape[0] // lanes
    low = part.dtype
    return pl.pallas_call(
        functools.partial(scatter_lanes_kernel, levels),
        out_shape=jax.ShapeDtypeStruct((rows, width), jnp.float32),
        in_specs=[pl.BlockSpec(memory_space=pltpu.VMEM)],
        out_specs=pl.BlockSpec(memory_space=pltpu.VMEM),
        scratch_shapes=[
            pltpu.VMEM((2, rows, width), low),
            pltpu.VMEM((rows, width), low),
            pltpu.VMEM((rows, width), low),
            pltpu.SemaphoreType.DMA((5,)),
            pltpu.SemaphoreType.DMA((5,)),
        ],
        compiler_params=pltpu.CompilerParams(collective_id=ident, has_side_effects=True),
        name="scatter_lanes",
    )(part.reshape(lanes, rows, width))


def scatter_last_kernel(
    levels, qkv, wout, small, parts, qkv_out, wout_out, small_out, gu_out, down_out,
    q_load, w_load, q_y, w_y, q_z, w_z, q_tx, w_tx, s_y, s_tx,
    load_sem, y_send, y_recv, z_send, z_recv, s_send, s_recv,
):
    place = Place(levels)
    z, y, x, c = place.z, place.y, place.x, place.c
    top = levels - 1
    x_dev, y_dev, c_dev = place.device(x=1 - x), place.device(y=1 - y), place.device(c=1 - c)
    out_width = w_y.shape[2]

    def remote(sends, recvs, where, ref, dst, device):
        return pltpu.make_async_remote_copy(
            src_ref=ref,
            dst_ref=dst,
            send_sem=sends.at[where],
            recv_sem=recvs.at[where],
            device_id=device,
            device_id_type=MESH_ID,
        )

    def block(level, yy):
        spot = level * 2 + yy
        return [qkv.at[k, spot] for k in range(3)] + [lane_block(wout, spot, out_width)]

    def pieces(q, w, level):
        return [q.at[level, k] for k in range(3)] + [w.at[level]]

    def load(level, i):
        ref = block(level, y)[i]
        dst = pieces(q_load, w_load, level)[i]
        return pltpu.make_async_copy(ref, dst, load_sem.at[i, level])

    def across(level, i):
        ref = block(level, 1 - y)[i]
        dst = pieces(q_y, w_y, level)[i]
        return remote(y_send, y_recv, (i, level), ref, dst, y_dev)

    def along(kind, level, slot, device, i):
        ref, dst = pieces(q_tx, w_tx, level)[i], pieces(q_z, w_z, slot)[i]
        return remote(z_send, z_recv, (kind, i, level), ref, dst, device)

    greet(place, [x_dev, y_dev, c_dev], True)

    s_first = remote(s_send, s_recv, 0, small.at[1 - c], s_y.at[0], c_dev)
    s_first.start()
    s_first.wait_recv()
    s_tx[0] = small[c] + s_y[0]
    s_yy = remote(s_send, s_recv, 1, s_tx.at[0], s_y.at[1], y_dev)
    s_yy.start()

    def each_level(action):
        for t in range(levels - 1, 0, -1):
            @pl.when(z - t >= 0)
            def _():
                action(z - t)

            @pl.when(z + t <= top)
            def _():
                action(z + t)

        action(z)

    def begin(level):
        for i in range(4):
            across(level, i).start()
            load(level, i).start()

    each_level(begin)

    s_yy.wait_recv()
    s_tx[2 + z] = s_tx[0] + s_y[1]

    def share(kind, level):
        ref = s_tx.at[2 + level]
        target = place.device(z=z + 1) if kind == 0 else place.device(z=z - 1)
        return remote(s_send, s_recv, 4 + kind * levels + level, ref, ref, target)

    @pl.when(z < top)
    def _():
        share(0, z).start()

    @pl.when(z > 0)
    def _():
        share(1, z).start()

    for t in range(1, levels):
        @pl.when(z - t >= 0)
        def _():
            share(0, z - t).wait_recv()

            @pl.when(z < top)
            def _():
                share(0, z - t).start()

        @pl.when(z + t <= top)
        def _():
            share(1, z + t).wait_recv()

            @pl.when(z > 0)
            def _():
                share(1, z + t).start()

    whole = s_tx[2]
    for level in range(1, levels):
        whole = whole + s_tx[2 + level]
    s_tx[1] = whole
    s_x = remote(s_send, s_recv, 2, s_tx.at[1], s_y.at[2], x_dev)
    s_x.start()

    units = parts.shape[3]
    for i in range(parts.shape[0]):
        span = slice(i * units, (i + 1) * units)
        for k in range(2):
            gu_out[k, :, span] = parts[i, k].astype(jnp.float32)
        down_out[span] = parts[i, 2].astype(jnp.float32).T

    def strips(ref, action):
        def step(i, carry):
            rows = pl.ds(pl.multiple_of(i * 16, 16), 16)
            ref[rows] = action(rows).astype(ref.dtype)
            return carry
        lax.fori_loop(0, ref.shape[0] // 16, step, 0)

    def f32(ref, rows):
        return ref[rows].astype(jnp.float32)

    def pass_on(level, kind, first, target, slot):
        mine, theirs = pieces(q_load, w_load, level), pieces(q_y, w_y, level)
        ahead, results = pieces(q_z, w_z, level), pieces(q_tx, w_tx, level)
        for i in range(4):
            load(level, i).wait()
            across(level, i).wait_recv()

            @pl.when(first)
            def _():
                strips(results[i], lambda rows: f32(mine[i], rows) + f32(theirs[i], rows))

            @pl.when(jnp.logical_not(first))
            def _():
                along(kind, level, level, c_dev, i).wait_recv()
                strips(
                    results[i],
                    lambda rows: f32(mine[i], rows) + f32(theirs[i], rows) + f32(ahead[i], rows),
                )
            along(kind, level, slot, target, i).start()

    for t in range(levels - 1, 0, -1):
        @pl.when(z + t <= top)
        def _():
            pass_on(z + t, 0, z == 0, place.device(z=z + 1), z + t)

        @pl.when(z - t >= 0)
        def _():
            slot = (z - t) if t > 1 else levels
            pass_on(z - t, 1, z == top, place.device(z=z - 1), slot)

        if t == levels - 1:
            s_x.wait_recv()
            small_out[c] = s_tx[1] + s_y[2]
            s_last = remote(s_send, s_recv, 3, small_out.at[c], small_out.at[c], c_dev)
            s_last.start()

    results = [qkv_out.at[k] for k in range(3)] + [wout_out]
    mine, theirs = pieces(q_load, w_load, z), pieces(q_y, w_y, z)
    for i in range(4):
        load(z, i).wait()
        across(z, i).wait_recv()
        strips(results[i], lambda rows: f32(mine[i], rows) + f32(theirs[i], rows))
    for kind, here, slot in ((0, z > 0, z), (1, z < top, levels)):
        ahead = pieces(q_z, w_z, slot)

        @pl.when(here)
        def _():
            for i in range(4):
                along(kind, z, slot, c_dev, i).wait_recv()
                strips(results[i], lambda rows: results[i][rows] + f32(ahead[i], rows))

    remote(s_send, s_recv, 3, small_out.at[1 - c], small_out.at[1 - c], c_dev).wait_recv()
    for one in (s_first, s_x, s_yy, s_last):
        one.wait_send()
    for level in range(levels):
        for i in range(4):
            across(level, i).wait_send()

        @pl.when(level > z)
        def _():
            for i in range(4):
                along(0, level, level, c_dev, i).wait_send()

        @pl.when(level < z)
        def _():
            for i in range(4):
                along(1, level, level, c_dev, i).wait_send()

        @pl.when((z < top) & (level <= z))
        def _():
            share(0, level).wait_send()

        @pl.when((z > 0) & (level >= z))
        def _():
            share(1, level).wait_send()


def scatter_last(grad_qkv, grad_wout, small, parts, levels, ident):
    wide = parts.shape[0] * parts.shape[3]
    spots = levels * 2
    depth, width = grad_qkv.shape[1] // spots, grad_qkv.shape[2]
    out_rows, out_width = grad_wout.shape[0], grad_wout.shape[1] // spots
    low = grad_qkv.dtype
    vmem = pl.BlockSpec(memory_space=pltpu.VMEM)
    hbm = pl.BlockSpec(memory_space=pl.ANY)

    def pair(count):
        return [
            pltpu.VMEM((count, 3, depth, width), low),
            pltpu.VMEM((count, out_rows, out_width), low),
        ]

    return pl.pallas_call(
        functools.partial(scatter_last_kernel, levels),
        out_shape=[
            jax.ShapeDtypeStruct((3, depth, width), jnp.float32),
            jax.ShapeDtypeStruct((out_rows, out_width), jnp.float32),
            jax.ShapeDtypeStruct(small.shape, jnp.float32),
            jax.ShapeDtypeStruct((2, parts.shape[2], wide), jnp.float32),
            jax.ShapeDtypeStruct((wide, parts.shape[2]), jnp.float32),
        ],
        in_specs=[hbm, hbm, vmem, vmem],
        out_specs=[vmem] * 5,
        scratch_shapes=pair(levels)
        + pair(levels)
        + pair(levels + 1)
        + pair(levels)
        + [
            pltpu.VMEM((3,) + small.shape[1:], jnp.float32),
            pltpu.VMEM((2 + levels,) + small.shape[1:], jnp.float32),
            pltpu.SemaphoreType.DMA((4, levels)),
            pltpu.SemaphoreType.DMA((4, levels)),
            pltpu.SemaphoreType.DMA((4, levels)),
            pltpu.SemaphoreType.DMA((2, 4, levels)),
            pltpu.SemaphoreType.DMA((2, 4, levels)),
            pltpu.SemaphoreType.DMA((4 + 2 * levels,)),
            pltpu.SemaphoreType.DMA((4 + 2 * levels,)),
        ],
        compiler_params=pltpu.CompilerParams(
            collective_id=ident, has_side_effects=True, vmem_limit_bytes=48 * 2**20
        ),
        name="scatter_last",
    )(grad_qkv.reshape(3, spots, depth, width), grad_wout, small, parts)


PAIR = 256
SIDE = 128


def mul(a, b, ca, cb):
    return lax.dot_general(
        a, b, (((ca,), (cb,)), ((), ())), preferred_element_type=jnp.float32
    )


def swish_parts(gate, up):
    sig = jax.nn.sigmoid(gate)
    silu = gate * sig
    return silu * up, up * sig * (1.0 + gate * (1.0 - sig)), silu


def chosen(slot_row, capacity):
    ids = lax.broadcasted_iota(jnp.int32, (capacity, slot_row.shape[1]), 0)
    return (ids == slot_row).astype(jnp.float32).astype(jnp.bfloat16)


def rows_in_kernel(
    capacity, experts, spare, x, parts, extra, slots,
    hid, to_gate, to_up, stats, taken, weights, down,
):
    units = parts.shape[3]

    @pl.when(pl.program_id(0) == 0)
    def _():
        weights[...] = jnp.zeros_like(weights)
        down[...] = jnp.zeros_like(down)
        weights[:, PAIR + SIDE :] = extra[...]
        depth = parts.shape[2]
        for i in range(parts.shape[0]):
            span = slice(i * depth, (i + 1) * depth)
            weights[span, :units] = parts[i, 0]
            weights[span, PAIR : PAIR + units] = parts[i, 1]
            down[span, :units] = parts[i, 2]

    acc = jnp.dot(x[...], weights[...], preferred_element_type=jnp.float32)
    gate, up = acc[:, :PAIR], acc[:, PAIR:]
    hidden, by_gate, by_up = swish_parts(gate, up)
    hid[...] = hidden.astype(hid.dtype)
    to_gate[...] = by_gate
    to_up[...] = by_up
    side = up[:, SIDE:]
    lane = lax.broadcasted_iota(jnp.int32, side.shape, 1)
    routed = (lane >= spare) & (lane < spare + experts)
    powers = jnp.where(routed, jnp.exp(jnp.where(routed, side, 0.0)), 0.0)
    probs = powers / jnp.sum(powers, axis=1, keepdims=True)
    gated = (lane >= spare + experts) & (lane < spare + experts + 3)
    sig = jax.nn.sigmoid(jnp.sum(jnp.where(gated, side, 0.0), axis=1, keepdims=True))
    stats[...] = jnp.where(routed, probs, jnp.where(gated, sig, 0.0))
    tokens = slots.shape[2]
    for b in range(slots.shape[1]):
        pick = chosen(slots[0, b : b + 1], capacity)
        rows = jnp.dot(
            pick, x[b * tokens : (b + 1) * tokens], preferred_element_type=jnp.float32
        )
        taken[b * capacity : (b + 1) * capacity] = rows.astype(taken.dtype)


def resident(shape):
    zeros = (0,) * len(shape)
    return pl.BlockSpec(shape, lambda i: zeros, pipeline_mode=pl.Buffered(1))


def tiled(rows, width):
    return pl.BlockSpec((rows, width), lambda i: (i, 0))


def stacked(*shape):
    rest = (0,) * len(shape)
    return pl.BlockSpec((1,) + shape, lambda i: (i,) + rest)


def cost(*products):
    return pl.CostEstimate(
        flops=sum(2 * m * k * n for m, k, n in products),
        bytes_accessed=sum(2 * (m * k + k * n + m * n) for m, k, n in products),
        transcendentals=0,
    )


def params():
    return pltpu.CompilerParams(vmem_limit_bytes=60 * 2**20)


def forward_kernel(
    levels, capacity, experts, spare, tiles, x, parts, extra, slots, w_gu, w_down, late,
    hid, to_gate, to_up, stats, taken_out, weights, down, e_hid, e_gate, e_up, e_out, late_all,
    taken, own_sem, send_sems, recv_sems,
):
    step = pl.program_id(0)
    comm = gather_steps(levels, [late], [late_all], own_sem, send_sems, recv_sems)

    @pl.when(step == 0)
    def _():
        comm[0]()

    size = slots.shape[1] * capacity

    @pl.when(step < tiles)
    def _():
        rows_in_kernel(
            capacity, experts, spare, x, parts, extra, slots,
            hid, to_gate, to_up, stats, taken_out, weights, down,
        )
        taken[pl.ds(pl.multiple_of(step * size, size), size)] = taken_out[...]

    @pl.when(step >= tiles)
    def _():
        tile = e_out.shape[0]
        first = pl.multiple_of((step - tiles) * tile, tile)
        rows = taken[pl.ds(first, tile)]
        gate = jnp.dot(rows, w_gu[0], preferred_element_type=jnp.float32)
        up = jnp.dot(rows, w_gu[1], preferred_element_type=jnp.float32)
        hidden, by_gate, by_up = swish_parts(gate, up)
        low = hidden.astype(e_hid.dtype)
        e_hid[...] = low
        e_gate[...] = by_gate
        e_up[...] = by_up
        e_out[...] = jnp.dot(low, w_down[...], preferred_element_type=jnp.float32).astype(
            e_out.dtype
        )

    total = pl.num_programs(0)
    times = (3, 8, 9, 10, 11)
    for i, action in enumerate(comm[1:-1]):
        at = jnp.minimum(times[min(i, len(times) - 1)], total - 1)

        @pl.when(step == at)
        def _():
            action()

    @pl.when(step == total - 1)
    def _():
        comm[-1]()


def forward(x, parts, extra, slots, w_gu, w_down, late, capacity, experts, spare, levels, ident):
    count, tokens = slots.shape
    rows, width = x.shape
    units = w_down.shape[0]
    per = 4
    tile = per * tokens
    tiles = rows // tile
    e_rows, e_tile = count * capacity, 256

    def early(*shape):
        rest = (0,) * (len(shape) - 1)
        return pl.BlockSpec(shape, lambda i: (jnp.minimum(i, tiles - 1),) + rest)

    def after(*shape):
        rest = (0,) * (len(shape) - 1)
        return pl.BlockSpec(shape, lambda i: (jnp.maximum(i - tiles, 0),) + rest)

    hbm = pl.BlockSpec(memory_space=pl.ANY)
    low, wide = jnp.bfloat16, jnp.float32
    sems = (11, levels, 1)
    return pl.pallas_call(
        functools.partial(forward_kernel, levels, capacity, experts, spare, tiles),
        grid=(tiles + e_rows // e_tile,),
        in_specs=[
            early(tile, width),
            resident(parts.shape),
            resident(extra.shape),
            early(1, per, tokens),
            resident(w_gu.shape),
            resident(w_down.shape),
            hbm,
        ],
        out_specs=[
            early(tile, PAIR),
            early(tile, PAIR),
            early(tile, PAIR),
            early(tile, PAIR - SIDE),
            early(per * capacity, width),
            resident((width, 2 * PAIR)),
            resident((width, PAIR)),
            after(e_tile, units),
            after(e_tile, units),
            after(e_tile, units),
            after(e_tile, width),
            hbm,
        ],
        out_shape=[
            jax.ShapeDtypeStruct((rows, PAIR), low),
            jax.ShapeDtypeStruct((rows, PAIR), wide),
            jax.ShapeDtypeStruct((rows, PAIR), wide),
            jax.ShapeDtypeStruct((rows, PAIR - SIDE), wide),
            jax.ShapeDtypeStruct((e_rows, width), low),
            jax.ShapeDtypeStruct((width, 2 * PAIR), low),
            jax.ShapeDtypeStruct((width, PAIR), low),
            jax.ShapeDtypeStruct((e_rows, units), low),
            jax.ShapeDtypeStruct((e_rows, units), wide),
            jax.ShapeDtypeStruct((e_rows, units), wide),
            jax.ShapeDtypeStruct((e_rows, width), low),
            jax.ShapeDtypeStruct((count,) + late.shape, late.dtype),
        ],
        scratch_shapes=[
            pltpu.VMEM((e_rows, width), low),
            pltpu.SemaphoreType.DMA((1,)),
            pltpu.SemaphoreType.DMA(sems),
            pltpu.SemaphoreType.DMA(sems),
        ],
        compiler_params=pltpu.CompilerParams(
            collective_id=ident, has_side_effects=True, vmem_limit_bytes=60 * 2**20
        ),
        cost_estimate=cost(
            (rows, width, 2 * PAIR), (e_rows, width, 2 * units), (e_rows, units, width)
        ),
        name="forward",
    )(x, parts, extra, slots.reshape(count // per, per, tokens), w_gu, w_down, late)


def rows_out_kernel(
    capacity, lane, hid, w_down, stats, slots, share, routed, grad, out, dots
):
    tokens = slots.shape[2]
    whole = mul(hid[...], w_down[...], 1, 1)
    for b in range(slots.shape[1]):
        span = slice(b * tokens, (b + 1) * tokens)
        here = slice(b * capacity, (b + 1) * capacity)
        part = whole[span]
        pick = chosen(slots[0, b : b + 1], capacity)
        weighted = (share[here] * routed[here].astype(jnp.float32)).astype(jnp.bfloat16)
        spread = mul(pick, weighted, 0, 0)
        out[span] = (stats[span, lane : lane + 1] * part + spread).astype(out.dtype)
        inner = jnp.sum(grad[span].astype(jnp.float32) * part, axis=1, keepdims=True)
        dots[span] = jnp.broadcast_to(inner, (tokens, dots.shape[1]))


def rows_out(hid, w_down, stats, slots, share, routed, grad, capacity, lane):
    count, tokens = slots.shape
    rows, width = count * tokens, routed.shape[1]
    per = 4
    tile = per * tokens
    return pl.pallas_call(
        functools.partial(rows_out_kernel, capacity, lane),
        grid=(rows // tile,),
        in_specs=[
            tiled(tile, PAIR),
            resident(w_down.shape),
            tiled(tile, stats.shape[1]),
            stacked(per, tokens),
            tiled(per * capacity, 1),
            tiled(per * capacity, width),
            tiled(tile, width),
        ],
        out_specs=[tiled(tile, width), tiled(tile, 128)],
        out_shape=[
            jax.ShapeDtypeStruct((rows, width), jnp.bfloat16),
            jax.ShapeDtypeStruct((rows, 128), jnp.float32),
        ],
        compiler_params=params(),
        cost_estimate=cost((rows, PAIR, width), (rows, capacity, width)),
        name="rows_out",
    )(hid, w_down, stats, slots.reshape(count // per, per, tokens), share, routed, grad)


def expert_back_kernel(
    capacity, grad, slots, share, out, to_gate, to_up, w_gu, w_down, dout, dgu, din, dots
):
    tokens = slots.shape[2]
    size = slots.shape[1]
    taken = []
    for b in range(size):
        pick = chosen(slots[0, b : b + 1], capacity)
        taken.append(
            jnp.dot(
                pick, grad[b * tokens : (b + 1) * tokens], preferred_element_type=jnp.float32
            )
        )
    rows = jnp.concatenate(taken, axis=0)
    inner = jnp.sum(rows * out[...].astype(jnp.float32), axis=1, keepdims=True)
    dots[...] = jnp.broadcast_to(inner, dots.shape)
    low = (share[...] * rows).astype(jnp.bfloat16)
    dout[...] = low
    dhid = mul(low, w_down[...], 1, 1)
    dgate = (dhid * to_gate[...]).astype(jnp.bfloat16)
    dup = (dhid * to_up[...]).astype(jnp.bfloat16)
    dgu[0] = dgate
    dgu[1] = dup
    din[...] = (mul(dgate, w_gu[0], 1, 1) + mul(dup, w_gu[1], 1, 1)).astype(din.dtype)


def expert_back(grad, slots, share, out, to_gate, to_up, w_gu, w_down, capacity):
    count, tokens = slots.shape
    rows, width = out.shape
    units = w_down.shape[0]
    tile = 256
    per = tile // capacity
    return pl.pallas_call(
        functools.partial(expert_back_kernel, capacity),
        grid=(rows // tile,),
        in_specs=[
            tiled(per * tokens, width),
            stacked(per, tokens),
            tiled(tile, 1),
            tiled(tile, width),
            tiled(tile, units),
            tiled(tile, units),
            resident(w_gu.shape),
            resident(w_down.shape),
        ],
        out_specs=[
            tiled(tile, width),
            pl.BlockSpec((2, tile, units), lambda i: (0, i, 0)),
            tiled(tile, width),
            tiled(tile, 128),
        ],
        out_shape=[
            jax.ShapeDtypeStruct((rows, width), jnp.bfloat16),
            jax.ShapeDtypeStruct((2, rows, units), jnp.bfloat16),
            jax.ShapeDtypeStruct((rows, width), jnp.bfloat16),
            jax.ShapeDtypeStruct((rows, 128), jnp.float32),
        ],
        compiler_params=params(),
        cost_estimate=cost((rows, width, units), (rows, 2 * units, width)),
        name="expert_back",
    )(
        grad,
        slots.reshape(count // per, per, tokens),
        share,
        out,
        to_gate,
        to_up,
        w_gu,
        w_down,
    )


def rows_back_kernel(
    levels, capacity, lane, grad, x, stats, hid, to_gate, to_up, slots, din, weights, w_down, part,
    out, grad_parts, own, sum_weights, sum_down, *scratch
):
    step = pl.program_id(0)
    comm = scatter_steps(levels, part, own, *scratch)

    @pl.when(step == 0)
    def _():
        comm[0]()

    @pl.when(step == 0)
    def _():
        sum_weights[...] = jnp.zeros_like(sum_weights)
        sum_down[...] = jnp.zeros_like(sum_down)

    low = (stats[:, lane : lane + 1] * grad[...].astype(jnp.float32)).astype(jnp.bfloat16)
    dhid = mul(low, w_down[...], 1, 0)
    dgate = (dhid * to_gate[...]).astype(jnp.bfloat16)
    dup = (dhid * to_up[...]).astype(jnp.bfloat16)
    both_grads = jnp.concatenate([dgate, dup], axis=1)
    sum_weights[...] += mul(both_grads, x[...], 0, 0)
    whole = mul(both_grads, weights[...], 1, 1)
    sum_down[...] += mul(hid[...], low, 0, 0)
    tokens = slots.shape[2]
    for b in range(slots.shape[1]):
        span = slice(b * tokens, (b + 1) * tokens)
        pick = chosen(slots[0, b : b + 1], capacity)
        back = whole[span]
        spread = mul(pick, din[b * capacity : (b + 1) * capacity], 0, 0)
        out[span] = (back + spread).astype(out.dtype)

    @pl.when(step == pl.num_programs(0) - 1)
    def _():
        depth, units = grad_parts.shape[2:]
        for i in range(grad_parts.shape[0]):
            span = slice(i * depth, (i + 1) * depth)
            grads = sum_weights[:, span].T.astype(grad_parts.dtype)
            grad_parts[i, 0] = grads[:, :units]
            grad_parts[i, 1] = grads[:, PAIR : PAIR + units]
            grad_parts[i, 2] = sum_down[:, span].T.astype(grad_parts.dtype)[:, :units]

    last = pl.num_programs(0) - 1
    for i, action in enumerate(comm[1:]):
        @pl.when(step == jnp.minimum(i, last))
        def _():
            action()


def rows_back(
    grad, x, stats, hid, to_gate, to_up, slots, din, weights, w_down, part, parts_shape,
    capacity, lane, levels, ident,
):
    count, tokens = slots.shape
    rows, width = x.shape
    per = 4
    tile = per * tokens
    return pl.pallas_call(
        functools.partial(rows_back_kernel, levels, capacity, lane),
        grid=(rows // tile,),
        in_specs=[
            tiled(tile, width),
            tiled(tile, width),
            tiled(tile, stats.shape[1]),
            tiled(tile, PAIR),
            tiled(tile, PAIR),
            tiled(tile, PAIR),
            stacked(per, tokens),
            tiled(per * capacity, width),
            resident(weights.shape),
            resident(w_down.shape),
            pl.BlockSpec(memory_space=pl.ANY),
        ],
        out_specs=[tiled(tile, width), resident(parts_shape), resident(part.shape[1:])],
        out_shape=[
            jax.ShapeDtypeStruct((rows, width), jnp.bfloat16),
            jax.ShapeDtypeStruct(parts_shape, jnp.bfloat16),
            jax.ShapeDtypeStruct(part.shape[1:], jnp.float32),
        ],
        scratch_shapes=[
            pltpu.VMEM(weights.shape[::-1], jnp.float32),
            pltpu.VMEM(w_down.shape[::-1], jnp.float32),
        ]
        + scatter_scratch(levels, part.shape[1], width, part.dtype),
        compiler_params=pltpu.CompilerParams(
            collective_id=ident, has_side_effects=True, vmem_limit_bytes=67043328
        ),
        cost_estimate=cost((rows, width, PAIR), (rows, 2 * PAIR, width), (2 * PAIR, rows, width), (PAIR, rows, width)),
        name="rows_back",
    )(
        grad, x, stats, hid, to_gate, to_up,
        slots.reshape(count // per, per, tokens), din, weights, w_down, part,
    )


def gu_grad_kernel(x, dgu, out):
    rows = x[...].T
    for i in range(2):
        out[i] = jnp.dot(rows, dgu[i], preferred_element_type=jnp.float32)


def down_grad_kernel(hid, dout, out, turned):
    @pl.when(pl.program_id(0) == 0)
    def _():
        turned[...] = hid[...].T

    out[...] = jnp.dot(turned[...], dout[...], preferred_element_type=jnp.float32)


def expert_weight_grads(x, dgu, hid, dout):
    rows, width = x.shape
    units = hid.shape[1]
    tile = 256
    grad_gu = pl.pallas_call(
        gu_grad_kernel,
        grid=(width // tile,),
        in_specs=[pl.BlockSpec((rows, tile), lambda i: (0, i)), resident(dgu.shape)],
        out_specs=pl.BlockSpec((2, tile, units), lambda i: (0, i, 0)),
        out_shape=jax.ShapeDtypeStruct((2, width, units), jnp.float32),
        compiler_params=params(),
        cost_estimate=cost((width, rows, 2 * units)),
        name="expert_gu_grad",
    )(x, dgu)
    grad_down = pl.pallas_call(
        down_grad_kernel,
        grid=(width // tile,),
        in_specs=[resident(hid.shape), pl.BlockSpec((rows, tile), lambda i: (0, i))],
        out_specs=pl.BlockSpec((units, tile), lambda i: (0, i)),
        out_shape=jax.ShapeDtypeStruct((units, width), jnp.float32),
        scratch_shapes=[pltpu.VMEM((units, rows), jnp.bfloat16)],
        compiler_params=params(),
        cost_estimate=cost((units, rows, width)),
        name="expert_down_grad",
    )(hid, dout)
    return grad_gu, grad_down


def rope_tables(length, head_width):
    half_width = head_width // 2
    inverse = rope_base ** (-(jnp.arange(half_width, dtype=jnp.float32) * 2.0 / head_width))
    angles = jnp.arange(length, dtype=jnp.float32)[:, None] * inverse[None, :]
    angles = jnp.concatenate([angles, angles], axis=1)
    return (jnp.cos(angles), jnp.sin(angles))


def rotate(values, cosine, sine_tab):
    half_width = values.shape[-1] // 2
    turned = jnp.concatenate([-values[..., half_width:], values[..., :half_width]], axis=-1)
    return values * cosine[:, None, :] + turned * sine_tab[:, None, :]


def rotate_back(grad_vals, cosine, sine_tab):
    half_width = grad_vals.shape[-1] // 2
    scaled = grad_vals * sine_tab[:, None, :]
    turned = jnp.concatenate([scaled[..., half_width:], -scaled[..., :half_width]], axis=-1)
    return grad_vals * cosine[:, None, :] + turned


def norm_rows(values):
    scale_rows = lax.rsqrt(jnp.mean(values * values, axis=-1, keepdims=True) + eps)
    return (values * scale_rows, scale_rows)


def norm_back(grad_normed, unit_rows, scale_rows, gain_vec):
    inner_term = grad_normed * gain_vec
    return scale_rows * (
        inner_term - unit_rows * jnp.mean(inner_term * unit_rows, axis=-1, keepdims=True)
    )


def heads_dot(a, b, ca, cb, ha, hb):
    return lax.dot_general(
        a, b, (((ca,), (cb,)), ((ha,), (hb,))), preferred_element_type=jnp.float32
    )


def masked_scores(query_blk, keys_low, first_row, factor):
    scores = heads_dot(query_blk, keys_low, 2, 2, 1, 1) * factor
    row_ids = first_row + jnp.arange(query_blk.shape[0], dtype=jnp.int32)
    col_ids = jnp.arange(keys_low.shape[0], dtype=jnp.int32)
    causal = col_ids[None, :] <= row_ids[:, None]
    return jnp.where(causal[None], scores, -jnp.inf)


def silu_pair(gate_up):
    sig_gate = jax.nn.sigmoid(gate_up[0])
    return (gate_up[0] * sig_gate, sig_gate)


def swiglu_back(grad_hid, gate_up):
    silu_gate, sig_gate = silu_pair(gate_up)
    grad_gate = grad_hid * gate_up[1] * sig_gate * (1.0 + gate_up[0] * (1.0 - sig_gate))
    grad_up = grad_hid * silu_gate
    return jnp.stack([grad_gate, grad_up], axis=0).astype(jnp.bfloat16)


def pair_mul(rows, weights):
    return jnp.stack([mul(rows, w, 1, 0) for w in weights])


class Attention:
    def __init__(self, normed_group, full_qkv, b_qkv):
        self.normed, self.weights = normed_group, full_qkv
        self.length, self.width = normed_group.shape[0], full_qkv.shape[2]
        heads = self.width // HEAD_DIM
        self.factor = HEAD_DIM ** (-0.5)
        projected = pair_mul(normed_group, full_qkv) + b_qkv[:, None, :]
        self.cosine, self.sine_tab = rope_tables(self.length, HEAD_DIM)
        split = projected.reshape(3, self.length, heads, HEAD_DIM)
        self.queries = rotate(split[0], self.cosine, self.sine_tab).astype(jnp.bfloat16)
        self.keys = rotate(split[1], self.cosine, self.sine_tab).astype(jnp.bfloat16)
        self.values = split[2].astype(jnp.bfloat16)
        scores = masked_scores(self.queries, self.keys, 0, self.factor)
        row_max = jnp.max(scores, axis=-1, keepdims=True)
        weights = jnp.exp(scores - row_max)
        row_sum = jnp.sum(weights, axis=-1, keepdims=True)
        probs_low = (weights / row_sum).astype(jnp.bfloat16)
        mixed = heads_dot(probs_low, self.values, 2, 0, 0, 1).astype(jnp.bfloat16)
        self.mixed = mixed.swapaxes(0, 1).reshape(self.length, self.width)
        self.logsum = row_max + jnp.log(row_sum)

    def back(self, grad_mixed):
        grad_mixed = grad_mixed.reshape(self.length, -1, HEAD_DIM)
        scores = masked_scores(self.queries, self.keys, 0, self.factor)
        soft_probs = jnp.exp(scores - self.logsum)
        probs_low = soft_probs.astype(jnp.bfloat16)
        grad_values = heads_dot(probs_low, grad_mixed, 1, 0, 0, 1)
        grad_probs = heads_dot(grad_mixed, self.values, 2, 2, 1, 1)
        grad_scores = soft_probs * (
            grad_probs - jnp.sum(soft_probs * grad_probs, axis=-1, keepdims=True)
        )
        low = grad_scores.astype(jnp.bfloat16)
        grad_queries = heads_dot(low, self.keys, 2, 0, 0, 1) * self.factor
        grad_keys = heads_dot(low, self.queries, 1, 0, 0, 1) * self.factor
        grad_proj = jnp.stack(
            [
                rotate_back(grad_queries.swapaxes(0, 1), self.cosine, self.sine_tab),
                rotate_back(grad_keys.swapaxes(0, 1), self.cosine, self.sine_tab),
                grad_values.swapaxes(0, 1),
            ]
        )
        grad_proj = grad_proj.reshape(3, self.length, self.width).astype(jnp.bfloat16)
        bias_sum = jnp.sum(grad_proj, axis=1, dtype=jnp.float32)
        grad_weights = jnp.stack(
            [mul(self.normed, grad, 0, 0).astype(jnp.bfloat16) for grad in grad_proj]
        )
        normed_part = sum(mul(g, w, 1, 1) for g, w in zip(grad_proj, self.weights))
        return bias_sum, grad_weights, normed_part


def local(
    tokens,
    gain_attn,
    w_qkv,
    b_qkv,
    w_out,
    gain_ffn,
    w_router,
    shared_gate,
    w_shared_gu,
    w_shared_down,
    w_expert_gu,
    w_expert_down,
    routes,
    grad_out,
):
    own_rows, model_width = tokens.shape
    spots, lanes = lax.axis_size(EXPERT), lax.axis_size(SHARD)
    levels, devices = spots // 2, spots * lanes
    me = lax.axis_index(both)
    local_width = w_qkv.shape[2]
    experts_all = w_router.shape[1]
    capacity = 2 * own_rows * TOPK // experts_all
    units = w_shared_down.shape[0] // spots

    x_own = tokens.astype(jnp.float32)
    unit_one, scale_one = norm_rows(x_own)
    normed_one = (unit_one * gain_attn).astype(jnp.bfloat16)
    full_qkv, full_out, normed_group = gather_first(w_qkv, w_out, normed_one, levels, lanes, 1)
    w_shared_gu, w_shared_down, normed_group = lax.optimization_barrier(
        (w_shared_gu, w_shared_down, normed_group)
    )
    parts = jnp.concatenate([w_shared_gu, w_shared_down.T[None]])
    parts = parts.reshape(3, -1, spots, units).transpose(2, 0, 1, 3)
    parts = lax.all_to_all(parts, EXPERT, 0, 0)
    gate_terms, rest = [], shared_gate
    for _ in range(3):
        term = lax.reduce_precision(rest, 8, 7)
        gate_terms.append(term.astype(jnp.bfloat16))
        rest = rest - term
    extra = jnp.concatenate([w_router, jnp.stack(gate_terms, axis=1)], axis=1)
    spare = units - SIDE
    extra = jnp.pad(extra, ((0, 0), (spare, PAIR - SIDE - spare - extra.shape[1])))
    gate_lane = spare + experts_all

    attention = Attention(normed_group, full_qkv, b_qkv)
    attn_own = scatter_lanes(mul(attention.mixed, full_out, 1, 0), levels, lanes, 2)
    hidden_own = x_own + attn_own
    unit_two, scale_two = norm_rows(hidden_own)
    normed_own = (unit_two * gain_ffn).astype(jnp.bfloat16)
    route_rows = jnp.zeros((16, own_rows), jnp.int32).at[:TOPK].set(routes.T)
    normed_own, route_rows, parts = lax.optimization_barrier((normed_own, route_rows, parts))
    normed_all, routes_all = gather_all([normed_own, route_rows], levels, devices, 3)

    hits = (routes_all.reshape(devices, 16, own_rows)[:, :TOPK] == me).any(axis=1)
    slots = jnp.where(hits, jnp.cumsum(hits.astype(jnp.int32), axis=1) - 1, -1)
    placed = slots[:, None, :] == jnp.arange(capacity, dtype=jnp.int32)[None, :, None]
    placed = placed.astype(jnp.float32)
    (
        shared_hid, shared_gate_by, shared_up_by, stats, received, slice_gu, slice_down,
        expert_hid, gate_by, up_by, expert_out, grad_all,
    ) = forward(
        normed_all, parts, extra, slots, w_expert_gu[0], w_expert_down[0], grad_out,
        capacity, experts_all, spare, levels, 8,
    )
    grad_all = grad_all.reshape(-1, model_width)
    mine = (jnp.arange(stats.shape[1], dtype=jnp.int32) == spare + me).astype(jnp.float32)
    prob_mine = jnp.sum(stats * mine, axis=1).reshape(devices, 1, own_rows)
    share = jnp.sum(placed * prob_mine, axis=2).reshape(-1, 1)
    ffn_part, gate_dots = rows_out(
        shared_hid, slice_down, stats, slots, share, expert_out, grad_all, capacity, gate_lane
    )

    expert_dout, expert_dgu, expert_din, slot_dots = expert_back(
        grad_all, slots, share, expert_out, gate_by, up_by, w_expert_gu[0], w_expert_down[0], capacity
    )
    row_dots = jnp.sum(placed * slot_dots[:, 0].reshape(devices, capacity, 1), axis=1)
    dots = jnp.stack([row_dots, gate_dots[:, 0].reshape(devices, own_rows)], axis=1)
    dots = lax.all_to_all(dots, both, split_axis=0, concat_axis=0, tiled=True)
    normed_part, grad_parts, ffn_own = rows_back(
        grad_all, normed_all, stats, shared_hid, shared_gate_by, shared_up_by, slots,
        expert_din, slice_gu, slice_down, ffn_part.reshape(devices, own_rows, model_width),
        parts.shape, capacity, gate_lane, levels, 9,
    )
    grad_expert_gu, grad_expert_down = expert_weight_grads(
        received, expert_dgu, expert_hid, expert_dout
    )
    grad_normed_own = scatter_all(
        normed_part.reshape(devices, own_rows, model_width), levels, 4
    )

    grad_normed_own, grad_parts = lax.optimization_barrier((grad_normed_own, grad_parts))
    grad_parts = lax.all_to_all(grad_parts, EXPERT, 0, 0)

    stats_own = lax.dynamic_slice_in_dim(stats, me * own_rows, own_rows, 0)
    probs_own = stats_own[:, spare : spare + experts_all]
    sig_own = stats_own[:, gate_lane]
    grad_own = grad_out.astype(jnp.float32)
    grad_router_probs = dots[:, 0, :].T
    grad_logits = probs_own * (
        grad_router_probs - jnp.sum(probs_own * grad_router_probs, axis=-1, keepdims=True)
    )
    logits_low = grad_logits.astype(jnp.bfloat16)
    grad_router = mul(normed_own, logits_low, 0, 0)
    grad_gate_logit = jnp.sum(dots[:, 1, :], axis=0) * sig_own * (1.0 - sig_own)
    grad_gate_vec = jnp.sum(normed_own.astype(jnp.float32) * grad_gate_logit[:, None], axis=0)
    grad_normed_own = (
        grad_normed_own
        + mul(logits_low, w_router, 1, 1)
        + grad_gate_logit[:, None] * shared_gate[None, :]
    )
    grad_hidden_own = grad_own + norm_back(grad_normed_own, unit_two, scale_two, gain_ffn)
    grad_gain_two = jnp.sum(grad_normed_own * unit_two, axis=0)
    grad_hidden_low = gather_lanes(grad_hidden_own.astype(jnp.bfloat16), levels, lanes, 5)

    grad_mixed = mul(grad_hidden_low, full_out, 1, 1).astype(jnp.bfloat16)
    grad_bias_local, grad_qkv, normed_one_part = attention.back(grad_mixed)
    grad_wout = mul(attention.mixed, grad_hidden_low, 0, 0).astype(jnp.bfloat16)
    grad_normed_one = scatter_lanes(normed_one_part.astype(jnp.bfloat16), levels, lanes, 6)
    grad_tokens = grad_hidden_own + norm_back(grad_normed_one, unit_one, scale_one, gain_attn)
    grad_gain_one = jnp.sum(grad_normed_one * unit_one, axis=0)
    grad_bias_full = lax.dynamic_update_slice_in_dim(
        jnp.zeros((3, model_width), jnp.float32),
        grad_bias_local,
        lax.axis_index(SHARD) * local_width,
        1,
    )
    small = jnp.concatenate(
        [
            grad_router.reshape(-1, model_width),
            grad_gain_one[None],
            grad_gain_two[None],
            grad_gate_vec[None],
            grad_bias_full,
        ]
    )
    small_rows = small.shape[0]
    small = jnp.pad(small, ((0, -small_rows % 16), (0, 0))).reshape(2, -1, model_width)
    qkv_grad_part, wout_grad_part, small, shared_grad_in, shared_grad_down = scatter_last(
        grad_qkv, grad_wout, small, grad_parts, levels, 7
    )
    result = (hidden_own + ffn_own).astype(jnp.bfloat16)
    small = small.reshape(-1, model_width)[:small_rows]
    router_total = small[:-6].reshape(model_width, experts_all)
    gain_one_total, gain_two_total, gate_total = small[-6], small[-5], small[-4]
    bias_total = small[-3:]

    return (
        result,
        grad_tokens,
        gain_one_total,
        qkv_grad_part,
        bias_total,
        wout_grad_part,
        gain_two_total,
        router_total,
        gate_total,
        shared_grad_in,
        shared_grad_down,
        grad_expert_gu[None],
        grad_expert_down[None],
    )


def local_wide(
    tokens,
    gain_attn,
    w_qkv,
    b_qkv,
    w_out,
    gain_ffn,
    w_router,
    shared_gate,
    w_shared_gu,
    w_shared_down,
    w_expert_gu,
    w_expert_down,
    routes,
    grad_out,
):
    own_rows, model_width = tokens.shape
    shard_pos = lax.axis_index(SHARD)
    local_width = w_qkv.shape[2]
    experts_all = w_router.shape[1]
    capacity = 2 * own_rows * TOPK // experts_all
    first_own = shard_pos * own_rows

    def route_rows(block):
        block = block.reshape(experts_all, capacity, model_width)
        block = lax.all_to_all(block, both, split_axis=0, concat_axis=0, tiled=True)
        return block.reshape(-1, model_width)

    def group_rows(rows):
        return lax.all_gather(rows, SHARD, axis=0, tiled=True)

    def own(values):
        return lax.dynamic_slice_in_dim(values, first_own, own_rows, 0)

    full_qkv, full_out, full_sgu, full_sdown = (
        lax.all_gather(w_qkv, EXPERT, axis=1, tiled=True),
        lax.all_gather(w_out, EXPERT, axis=1, tiled=True),
        lax.all_gather(w_shared_gu, EXPERT, axis=1, tiled=True),
        lax.all_gather(w_shared_down, EXPERT, axis=1, tiled=True),
    )
    x_own = tokens.astype(jnp.float32)
    unit_one, scale_one = norm_rows(x_own)
    normed_one = (unit_one * gain_attn).astype(jnp.bfloat16)
    x_group, normed_group = group_rows(tokens), group_rows(normed_one)
    attention = Attention(normed_group, full_qkv, b_qkv)
    attn_group = lax.psum(mul(attention.mixed, full_out, 1, 0), SHARD)
    hidden_group = x_group.astype(jnp.float32) + attn_group
    unit_two, scale_two = norm_rows(hidden_group)
    normed_two = (unit_two * gain_ffn).astype(jnp.bfloat16)
    gate_logit = jnp.dot(normed_two.astype(jnp.float32), shared_gate, precision=highest)
    gate_sig = jax.nn.sigmoid(gate_logit)
    shared_gu = pair_mul(normed_two, full_sgu)
    shared_silu, shared_sig = silu_pair(shared_gu)
    shared_hid = (shared_silu * shared_gu[1]).astype(jnp.bfloat16)
    shared_part = mul(shared_hid, full_sdown, 1, 0)
    shared_own = lax.psum_scatter(
        shared_part.astype(jnp.bfloat16), SHARD, scatter_dimension=0, tiled=True
    ).astype(jnp.float32)
    normed_own, sig_own, hidden_own = own(normed_two), own(gate_sig), own(hidden_group)
    router_exp = jnp.exp(mul(normed_own, w_router, 1, 0))
    router_probs = router_exp / jnp.sum(router_exp, axis=-1, keepdims=True)
    expert_ids = jnp.arange(experts_all, dtype=jnp.int32)
    route_hits = (routes[:, :, None] == expert_ids[None, None, :]).astype(jnp.float32)
    picked = jnp.sum(router_probs[:, None, :] * route_hits, axis=-1)
    flat_routes = routes.reshape(-1)
    matches = (flat_routes[:, None] == expert_ids[None, :]).astype(jnp.int32)
    ranks = jnp.sum((jnp.cumsum(matches, axis=0) - 1) * matches, axis=1)
    targets = flat_routes * capacity + ranks

    def in_slots(rows):
        empty = jnp.zeros((experts_all * capacity, model_width), jnp.bfloat16)
        return empty.at[targets].set(rows)

    def at_slots(rows):
        return rows[targets].reshape(own_rows, TOPK, model_width).astype(jnp.float32)

    received = route_rows(in_slots(jnp.repeat(normed_own, TOPK, axis=0)))
    expert_gu = pair_mul(received, w_expert_gu[0])
    expert_silu, expert_sig = silu_pair(expert_gu)
    expert_hid = (expert_silu * expert_gu[1]).astype(jnp.bfloat16)
    expert_out = mul(expert_hid, w_expert_down[0], 1, 0).astype(jnp.bfloat16)
    route_out = at_slots(route_rows(expert_out))
    routed_own = jnp.sum(route_out * picked[:, :, None], axis=1)
    result = (hidden_own + sig_own[:, None] * shared_own + routed_own).astype(jnp.bfloat16)
    grad_own = grad_out.astype(jnp.float32)
    route_grad = (
        (picked[:, :, None] * grad_own[:, None, :]).reshape(-1, model_width).astype(jnp.bfloat16)
    )
    grad_recv = route_rows(in_slots(route_grad))
    grad_expert_down = mul(expert_hid, grad_recv, 0, 0)
    grad_expert_hid = mul(grad_recv, w_expert_down[0], 1, 1)
    expert_dgu = swiglu_back(grad_expert_hid, expert_gu)
    grad_expert_gu = jnp.stack([mul(received, grad, 0, 0) for grad in expert_dgu])
    expert_din = sum(mul(g, w, 1, 1) for g, w in zip(expert_dgu, w_expert_gu[0]))
    grad_normed_own = jnp.sum(at_slots(route_rows(expert_din.astype(jnp.bfloat16))), axis=1)
    grad_picked = jnp.sum(route_out * grad_own[:, None, :], axis=-1)
    grad_router_probs = jnp.sum(grad_picked[:, :, None] * route_hits, axis=1)
    grad_logits = router_probs * (
        grad_router_probs - jnp.sum(router_probs * grad_router_probs, axis=-1, keepdims=True)
    )
    logits_low = grad_logits.astype(jnp.bfloat16)
    grad_router = mul(normed_own, logits_low, 0, 0)
    grad_normed_own = grad_normed_own + mul(logits_low, w_router, 1, 1)
    grad_gate_logit = jnp.sum(grad_own * shared_own, axis=-1) * sig_own * (1.0 - sig_own)
    grad_gate_vec = jnp.dot(
        grad_gate_logit, normed_own.astype(jnp.float32), precision=highest
    )
    grad_normed_own = grad_normed_own + grad_gate_logit[:, None] * shared_gate[None, :]
    grad_group_f = group_rows(grad_out).astype(jnp.float32)
    grad_shared_out = (gate_sig[:, None] * grad_group_f).astype(jnp.bfloat16)
    grad_sdown = mul(shared_hid, grad_shared_out, 0, 0)
    grad_shared_hid = mul(grad_shared_out, full_sdown, 1, 1)
    shared_dgu = swiglu_back(grad_shared_hid, shared_gu)
    grad_sgu = jnp.stack([mul(normed_two, grad, 0, 0) for grad in shared_dgu])
    normed_part = sum(mul(g, w, 1, 1) for g, w in zip(shared_dgu, full_sgu))
    normed_part = lax.dynamic_update_slice_in_dim(
        normed_part, own(normed_part) + grad_normed_own, first_own, 0
    )
    grad_normed_two = lax.psum(normed_part, SHARD)
    grad_hidden = grad_group_f + norm_back(grad_normed_two, unit_two, scale_two, gain_ffn)
    grad_gain_two = jnp.sum(own(grad_normed_two * unit_two), axis=0)
    grad_hidden_low = grad_hidden.astype(jnp.bfloat16)
    grad_wout = mul(attention.mixed, grad_hidden_low, 0, 0)
    grad_mixed = mul(grad_hidden_low, full_out, 1, 1).astype(jnp.bfloat16)
    grad_bias_local, grad_qkv, normed_one_part = attention.back(grad_mixed)
    grad_normed_one = lax.psum_scatter(
        normed_one_part.astype(jnp.bfloat16), SHARD, scatter_dimension=0, tiled=True
    ).astype(jnp.float32)
    grad_tokens = own(grad_hidden) + norm_back(grad_normed_one, unit_one, scale_one, gain_attn)
    grad_gain_one = jnp.sum(grad_normed_one * unit_one, axis=0)
    grad_bias_full = lax.dynamic_update_slice_in_dim(
        jnp.zeros((3, model_width), jnp.float32), grad_bias_local, shard_pos * local_width, 1
    )

    def weight_sum(grad):
        low = grad.astype(jnp.bfloat16)
        total = lax.psum_scatter(low, EXPERT, scatter_dimension=1, tiled=True)
        return total.astype(jnp.float32)

    router_total, gain_one_total, gain_two_total, gate_total, bias_total = lax.psum(
        (grad_router, grad_gain_one, grad_gain_two, grad_gate_vec, grad_bias_full), both
    )
    return (
        result,
        grad_tokens,
        gain_one_total,
        weight_sum(grad_qkv),
        bias_total,
        weight_sum(grad_wout),
        gain_two_total,
        router_total,
        gate_total,
        weight_sum(grad_sgu),
        weight_sum(grad_sdown),
        grad_expert_gu[None],
        grad_expert_down[None],
    )


def local_by_size(*args):
    spots, lanes = lax.axis_size(EXPERT), lax.axis_size(SHARD)
    w_router, w_shared_down = args[6], args[9]
    units = w_shared_down.shape[0] // spots
    side = units - SIDE + w_router.shape[1] + 3
    fits = lanes == 4 and spots % 2 == 0 and spots * lanes <= 64
    fits = fits and SIDE <= units <= PAIR and side <= PAIR - SIDE
    return local(*args) if fits else local_wide(*args)


def solution(mesh):
    rows, columns = P(both, None), P(None, EXPERT, SHARD)
    weights = P(both, None, None, None), P(both, None, None)
    return jax.shard_map(
        local_by_size,
        mesh=mesh,
        in_specs=(
            rows, P(), columns, P(None, SHARD), P(SHARD, EXPERT), P(), P(), P(),
            columns, P(SHARD, EXPERT), *weights, rows, rows,
        ),
        out_specs=(
            rows, rows, P(), columns, P(), P(SHARD, EXPERT), P(), P(), P(),
            columns, P(SHARD, EXPERT), *weights,
        ),
        check_vma=False,
    )
```

time: 1710 us -> 831 us (0.49)
  waiting for transfers between devices: 1260 us -> 0.01 us
  Pallas kernels: 0 us -> 694 us
  matrix products: 197 us -> 34 us
  local copies, waits for them, and re-layouts: 99.1 us -> 44.2 us
  blocking collectives: 43.5 us -> 0 us
  other arithmetic: 65.1 us -> 29.4 us
    pallas_call x0 -> x13, Pallas kernels: none -> 694 us  [the longest x1 108 us: scatter_last(): pl.pallas_call(functools.partial(scatter_last_kernel, levels), out_shape=...]
    all_to_all x4 -> x3, waiting for transfers between devices: 403 us -> 0.01 us  [the longest x1 0.01 us: local(): parts = lax.all_to_all(parts, EXPERT, 0, 0)]
    reduce_scatter x6 -> x0, waiting for transfers between devices: 387 us -> none  [the longest x1 151 us: local(): lax.psum_scatter(grad_sgu.astype(jnp.bfloat16), 'expert', scatter_dimensi...]
    psum x3 -> x0, waiting for transfers between devices: 294 us -> none  [the longest x1 129 us: local(): lax.psum((grad_router, grad_gain_one, grad_gain_two, grad_gate_vec, grad_...]
    all_gather x7 -> x0, waiting for transfers between devices: 176 us -> none  [the longest x1 102 us: local(): lax.all_gather(w_qkv, 'expert', axis=1, tiled=True)]
    dot_general x29 -> x20, matrix products: 197 us -> 34 us  [the longest x14 29.1 us: mul(): lax.dot_general(a, b, (((ca,), (cb,)), ((), ())), preferred_element_type=...]
    psum x1 -> x0, blocking collectives: 43.5 us -> none  [local(): lax.psum((grad_router, grad_gain_one, grad_gain_two, grad_gate_vec, grad_...]
    unnamed x114 -> x126, local copies, waits for them, and re-layouts: 44.9 us -> 16.2 us
  transfers between devices with their start and end apart: 20 -> 3, of which waited for: 16 -> 0; matrix products, arithmetic and copies ran while one was open for 19% -> 8% of each run, Pallas kernels for 0% -> 33%
where the time goes in v1:
time: 831 us; the launch traced here: 820 us
  Pallas kernels  694 us (84%)
  local copies, waits for them, and re-layouts  44.2 us (5%)
  matrix products  34 us (4%)
  other arithmetic  29.4 us (4%)
  starting transfers between devices  16.6 us (2%)
    pallas_call x1, Pallas kernels, scatter_last(): pl.pallas_call(functools.partial(scatter_last_kernel, levels), out_shape=...  108 us
    pallas_call x1, Pallas kernels, gather_first(): pl.pallas_call(functools.partial(gather_first_kernel, levels), out_shape=...  97.3 us
    pallas_call x1, Pallas kernels, rows_back(): pl.pallas_call(functools.partial(rows_back_kernel, levels, capacity, lane...  88.1 us
    pallas_call x1, Pallas kernels, forward(): pl.pallas_call(functools.partial(forward_kernel, levels, capacity, expert...  87.7 us
    pallas_call x1, Pallas kernels, scatter_all(): pl.pallas_call(functools.partial(scatter_kernel, levels), out_shape=jax.S...  80.5 us
    pallas_call x1, Pallas kernels, gather_all(): pl.pallas_call(functools.partial(gather_kernel, levels, size), out_shape=...  78.5 us
    pallas_call x2, Pallas kernels, scatter_lanes(): pl.pallas_call(functools.partial(scatter_lanes_kernel, levels), out_shape...  49.6 us
    pallas_call x1, Pallas kernels, expert_back(): pl.pallas_call(functools.partial(expert_back_kernel, capacity), grid=(row...  33.2 us
  transfers between devices with their start and end apart: 3, of which 0 were waited for; matrix products, arithmetic and copies ran while one was open for 8% of the time, Pallas kernels for 33%

profile of v1, /device:TPU:0, one launch (start us, length us, event | category | flops | bytes accessed | tf_op | source)
XLA Modules:
  0.0 820.2 jit_solution(205564222387095948)
XLA Ops:
  4.6 97.3 %gather_first.1 = (bf16[3,8,256,512]{3,2,1,0:T(8,128)(2,1)}, bf16[512,2048]{1,0:T(8,128)(2,1)}, bf16[4,128,2048]{2,1,0:T(8,128)(2,1)}) custom-call(bf16[3,256,512]{2,1,0:T(8,128)(2,1)} %qkv.1, bf16[512,256]{1,0:T(8,128)(2,1)} %wout.1, bf16[128,2048]{1,0:T(8,128)(2,1)} %fusion.17.rows), custom_call_target="tpu_custom_call" | custom-call | tf_op jit(solution)/shard_map/gather_first/pallas_call | solution.py:614
  105.4 4.8 all-to-all-start
  110.4 3.6 fusion.40
  126.6 4.9 fusion.5.part
  131.5 30.7 %scatter_lanes.2 = f32[128,2048]{1,0:T(8,128)} custom-call(f32[4,128,2048]{2,1,0:T(8,128)} %fusion.5.part), custom_call_target="tpu_custom_call" | custom-call | tf_op jit(solution)/shard_map/scatter_lanes/pallas_call | solution.py:761
  167.7 2.7 copy.112.parts
  170.5 78.5 %gather_all.1 = (bf16[32,128,2048]{2,1,0:T(8,128)(2,1)}, s32[32,16,128]{2,1,0:T(8,128)}) custom-call(bf16[128,2048]{1,0:T(8,128)(2,1)} %multiply_convert_fusion.1.refs_0_, s32[16,128]{1,0:T(8,128)} %scatter.4.refs_1_), custom_call_target="tpu_custom_call" | custom-call | tf_op jit(solution)/shard_map/gather_all/pallas_call | solution.py:250
  250.9 87.7 %forward.1 = (bf16[4096,256]{1,0:T(8,128)(2,1)}, f32[4096,256]{1,0:T(8,128)}, f32[4096,256]{1,0:T(8,128)}, f32[4096,128]{1,0:T(8,128)}, bf16[1024,2048]{1,0:T(8,...) custom-call(bf16[4096,2048]{1,0:T(8,128)(2,1)} %bitcast.176, ...), custom_call_target="tpu_custom_call" | custom-call | flops 26306674688 | bytes 57409536 | tf_op jit(solution)/shard_map/forward/pallas_call | solution.py:1190
  342.4 21.1 %rows_out.1 = (bf16[4096,2048]{1,0:T(8,128)(2,1)}, f32[4096,128]{1,0:T(8,128)}) custom-call(bf16[4096,256]{1,0:T(8,128)(2,1)} %get-tuple-element.77.hid, bf16[2048,256]{1,0:T(8,128)(2,1)} %get-tuple-element.85.w_down, f32[4096,128]{1,0:T(8,128)} %get-tuple-element.76.stats, s32[8,4,128]{2,1,0:T(4,128)} %bitcast.162, f32[1024,1]{1,0:T(8,128)} %reshape.277.share, ...), custom_call_target="tpu_custom_call" | custom-call | flops 4831838208 | bytes 37093376 | tf_op jit(solution)/shard_map/rows_out/pallas_call | solution.py:1268
  365.7 33.2 %expert_back.1 = (bf16[1024,2048]{1,0:T(8,128)(2,1)}, bf16[2,1024,1408]{2,1,0:T(8,128)(2,1)}, bf16[1024,2048]{1,0:T(8,128)(2,1)}, f32[1024,128]{1,0:T(8,128)}) custom-call(bf16[4096,2048]{1,0:T(8,128)(2,1)} %bitcast.125, s32[4,8,128]{2,1,0:T(8,128)} %bitcast.163, f32[1024,1]{1,0:T(8,128)} %reshape.277.share, ...), custom_call_target="tpu_custom_call" | custom-call | flops 17716740096 | bytes 34340864 | tf_op jit(solution)/shard_map/expert_back/pallas_call | solution.py:1323
  401.1 6.8 all-to-all-start.1
  407.9 19.2 %expert_gu_grad.1 = f32[2,2048,1408]{2,1,0:T(8,128)} custom-call(bf16[1024,2048]{1,0:T(8,128)(2,1)} %get-tuple-element.99.x, bf16[2,1024,1408]{2,1,0:T(8,128)(2,1)} %get-tuple-element.100.dgu), custom_call_target="tpu_custom_call" | custom-call | flops 11811160064 | bytes 21495808 | tf_op jit(solution)/shard_map/expert_gu_grad/pallas_call | solution.py:1476
  427.1 88.1 %rows_back.1 = (bf16[4096,2048]{1,0:T(8,128)(2,1)}, bf16[8,3,256,176]{3,2,1,0:T(8,128)(2,1)}, f32[128,2048]{1,0:T(8,128)}) custom-call(bf16[4096,2048]{1,0:T(8,128)(2,1)} %bitcast.126, bf16[4096,2048]{1,0:T(8,128)(2,1)} %bitcast.177, f32[4096,128]{1,0:T(8,128)} %get-tuple-element.76.stats, bf16[4096,256]{1,0:T(8,128)(2,1)} %get-tuple-element.77.hid, ...), custom_call_target="tpu_custom_call" | custom-call | flops 25769803776 | bytes 85983232 | tf_op jit(solution)/shard_map/rows_back/pallas_call | solution.py:1420
  515.1 13.2 %expert_down_grad.1 = f32[1408,2048]{1,0:T(8,128)} custom-call(bf16[1024,1408]{1,0:T(8,128)(2,1)} %get-tuple-element.101.hid, bf16[1024,2048]{1,0:T(8,128)(2,1)} %get-tuple-element.102.dout), custom_call_target="tpu_custom_call" | custom-call | flops 5905580032 | bytes 12845056 | tf_op jit(solution)/shard_map/expert_down_grad/pallas_call | solution.py:1486
  528.3 80.5 %scatter_all.1 = f32[128,2048]{1,0:T(8,128)} custom-call(bf16[32,128,2048]{2,1,0:T(8,128)(2,1)} %bitcast.127), custom_call_target="tpu_custom_call" | custom-call | tf_op jit(solution)/shard_map/scatter_all/pallas_call | solution.py:484
  611.4 4.9 all-to-all-start.2
  623.2 18.1 %gather_lanes.1 = bf16[4,128,2048]{2,1,0:T(8,128)(2,1)} custom-call(bf16[128,2048]{1,0:T(8,128)(2,1)} %fusion.39.rows), custom_call_target="tpu_custom_call" | custom-call | tf_op jit(solution)/shard_map/gather_lanes/pallas_call | solution.py:680
  641.3 3.0 convolution_convert_fusion.4
  655.0 2.6 add_convert_fusion
  657.7 18.8 %scatter_lanes.3 = f32[128,2048]{1,0:T(8,128)} custom-call(bf16[4,128,2048]{2,1,0:T(8,128)(2,1)} %bitcast.132), custom_call_target="tpu_custom_call" | custom-call | tf_op jit(solution)/shard_map/scatter_lanes/pallas_call | solution.py:761
  683.0 3.1 convolution_convert_fusion.1
  691.8 3.2 pad_maximum_fusion.qkv
  696.6 4.5 copy.125.parts
  701.1 107.6 %scatter_last.1 = (f32[3,256,512]{2,1,0:T(8,128)S(1)}, f32[512,256]{1,0:T(8,128)S(1)}, f32[2,24,2048]{2,1,0:T(8,128)S(1)}, f32[2,256,1408]{2,1,0:T(8,128)}, f32[1408,256]{1,0:T(8,128)S(1)}) custom-call(bf16[3,8,256,512]{3,2,1,0:T(8,128)(2,1)} %pad_maximum_fusion.qkv, bf16[512,2048]{1,0:T(8,128)(2,1)} %convolution_convert_fusion.wout, ...), custom_call_target="tpu_custom_call" | custom-call | tf_op jit(solution)/shard_map/scatter_last/pallas_call | solution.py:997
  (214 shorter events, 79.9 us)
Async XLA Ops:
  0.6 101.3 %copy-start.36 = (bf16[2,256,1408]{2,1,0:T(8,128)(2,1)S(1)}, bf16[2,256,1408]{2,1,0:T(8,128)(2,1)}, u32[]{:S(2)}) copy-start(bf16[2,256,1408]{2,1,0:T(8,128)(2,1)} %param.24) | copy-start | bytes 4325380
  105.4 62.3 %all-to-all-start = ((bf16[8,3,256,176]{2,3,1,0:T(8,128)(2,1)}), bf16[8,3,256,176]{2,3,1,0:T(8,128)(2,1)S(1)}, u32[]{:S(2)}, u32[]{:S(2)}) async-start(bf16[8,3,256,176]{2,3,1,0:T(8,128)(2,1)} %copy.110), calls=%async_computation | async-start | bytes 4325376 | tf_op jit(solution)/shard_map/all_to_all | solution.py:1647
  119.2 4.4 copy-start.31
  131.5 30.7 %copy-start.50 = (f32[2048]{0:T(1024)S(1)}, f32[2048]{0:T(1024)}, u32[]{:S(2)}) copy-start(f32[2048]{0:T(1024)} %param.23) | copy-start | bytes 24580
  131.5 30.8 %copy-start.40 = (bf16[2048,32]{0,1:T(8,128)(2,1)S(1)}, bf16[2048,32]{0,1:T(8,128)(2,1)}, u32[]{:S(2)}) copy-start(bf16[2048,32]{0,1:T(8,128)(2,1)} %param.22) | copy-start | bytes 393220
  131.5 31.2 %copy-start.57 = (s32[128,4]{0,1:T(4,128)S(1)}, s32[128,4]{0,1:T(4,128)}, u32[]{:S(2)}) copy-start(s32[128,4]{0,1:T(4,128)} %param.28) | copy-start | bytes 6148
  162.4 4.4 copy-start.46
  165.8 4.6 copy-start.53
  365.7 34.6 %copy-start.45 = (s32[32,128]{1,0:T(8,128)S(1)}, s32[32,128]{1,0:T(8,128)}, u32[]{:S(2)}) copy-start(s32[32,128]{1,0:T(8,128)} %add_select_fusion) | copy-start | bytes 49156
  401.1 210.3 %all-to-all-start.1 = ((f32[32,2,128]{2,1,0:T(2,128)}), f32[32,2,128]{2,1,0:T(2,128)}, u32[]{:S(2)}, u32[]{:S(2)}) async-start(f32[32,2,128]{2,1,0:T(2,128)} %copy.115), calls=%async_computation.1 | async-start | bytes 65536 | tf_op jit(solution)/shard_map/all_to_all | solution.py:1691
  528.3 80.5 %copy-start.28 = (bf16[8,3,256,176]{3,2,1,0:T(8,128)(2,1)S(1)}, bf16[8,3,256,176]{3,2,1,0:T(8,128)(2,1)}, u32[]{:S(2)}) copy-start(bf16[8,3,256,176]{3,2,1,0:T(8,128)(2,1)} %get-tuple-element.93) | copy-start | bytes 6488068
  611.4 8.1 copy-start.5
  611.4 8.1 copy-start.27
  611.4 8.1 copy-start.41
  611.4 8.2 copy-start.47
  611.4 8.2 copy-start.51
  611.4 8.2 copy-start.54
  611.4 85.2 %all-to-all-start.2 = ((bf16[8,3,256,176]{2,3,1,0:T(8,128)(2,1)}), bf16[8,3,256,176]{2,3,1,0:T(8,128)(2,1)}, u32[]{:S(2)}, u32[]{:S(2)}) async-start(bf16[8,3,256,176]{2,3,1,0:T(8,128)(2,1)} %copy.124), calls=%async_computation.2 | async-start | bytes 4325376 | tf_op jit(solution)/shard_map/all_to_all | solution.py:1705
  616.3 5.7 copy-start.34
  623.2 18.1 %copy-start.33 = (bf16[512,2048]{1,0:T(8,128)(2,1)S(1)}, bf16[512,2048]{1,0:T(8,128)(2,1)}, u32[]{:S(2)}) copy-start(bf16[512,2048]{1,0:T(8,128)(2,1)} %get-tuple-element.67) | copy-start | bytes 6291460
  648.9 5.9 copy-start.22
  657.7 18.8 %copy-start.13 = (bf16[128,2048]{1,0:T(8,128)(2,1)S(1)}, bf16[128,2048]{1,0:T(8,128)(2,1)}, u32[]{:S(2)}) copy-start(bf16[128,2048]{1,0:T(8,128)(2,1)} %multiply_convert_fusion.1.refs_0_) | copy-start | bytes 1572868
  678.7 3.7 copy-start.49
  678.7 3.7 copy-start.56
  (39 other events, 78.8 us)

commit v2 on v1

--- a/solution.py
+++ b/solution.py
@@ -1050,7 +1050,7 @@
 
 def rows_in_kernel(
     capacity, experts, spare, x, parts, extra, slots,
-    hid, to_gate, to_up, stats, taken, weights, down,
+    hid, to_gate, to_up, stats, taken, weights, down, share,
 ):
     units = parts.shape[3]
 
@@ -1080,6 +1080,7 @@
     gated = (lane >= spare + experts) & (lane < spare + experts + 3)
     sig = jax.nn.sigmoid(jnp.sum(jnp.where(gated, side, 0.0), axis=1, keepdims=True))
     stats[...] = jnp.where(routed, probs, jnp.where(gated, sig, 0.0))
+    mine = jnp.sum(jnp.where(lane == spare + lax.axis_index(both), probs, 0.0), axis=1, keepdims=True)
     tokens = slots.shape[2]
     for b in range(slots.shape[1]):
         pick = chosen(slots[0, b : b + 1], capacity)
@@ -1087,6 +1088,10 @@
             pick, x[b * tokens : (b + 1) * tokens], preferred_element_type=jnp.float32
         )
         taken[b * capacity : (b + 1) * capacity] = rows.astype(taken.dtype)
+        share[b * capacity : (b + 1) * capacity] = jnp.dot(
+            pick.astype(jnp.float32), mine[b * tokens : (b + 1) * tokens],
+            precision=highest, preferred_element_type=jnp.float32,
+        )
 
 
 def resident(shape):
@@ -1117,8 +1122,8 @@
 
 def forward_kernel(
     levels, capacity, experts, spare, tiles, x, parts, extra, slots, w_gu, w_down, late,
-    hid, to_gate, to_up, stats, taken_out, weights, down, e_hid, e_gate, e_up, e_out, late_all,
-    taken, own_sem, send_sems, recv_sems,
+    hid, to_gate, to_up, stats, taken_out, weights, down, e_hid, e_gate, e_up, e_out, share, part,
+    late_all, taken, hid_all, stats_all, share_all, own_sem, send_sems, recv_sems,
 ):
     step = pl.program_id(0)
     comm = gather_steps(levels, [late], [late_all], own_sem, send_sems, recv_sems)
@@ -1133,15 +1138,22 @@
     def _():
         rows_in_kernel(
             capacity, experts, spare, x, parts, extra, slots,
-            hid, to_gate, to_up, stats, taken_out, weights, down,
+            hid, to_gate, to_up, stats, taken_out, weights, down, share,
         )
-        taken[pl.ds(pl.multiple_of(step * size, size), size)] = taken_out[...]
-
-    @pl.when(step >= tiles)
+        here = pl.ds(pl.multiple_of(step * size, size), size)
+        taken[here] = taken_out[...]
+        share_all[here] = share[...]
+        here = pl.ds(pl.multiple_of(step * x.shape[0], x.shape[0]), x.shape[0])
+        hid_all[here] = hid[...]
+        stats_all[here] = stats[...]
+
+    e_tiles = taken.shape[0] // e_out.shape[0]
+
+    @pl.when((step >= tiles) & (step < tiles + e_tiles))
     def _():
         tile = e_out.shape[0]
-        first = pl.multiple_of((step - tiles) * tile, tile)
-        rows = taken[pl.ds(first, tile)]
+        here = pl.ds(pl.multiple_of((step - tiles) * tile, tile), tile)
+        rows = taken[here]
         gate = jnp.dot(rows, w_gu[0], preferred_element_type=jnp.float32)
         up = jnp.dot(rows, w_gu[1], preferred_element_type=jnp.float32)
         hidden, by_gate, by_up = swish_parts(gate, up)
@@ -1149,12 +1161,26 @@
         e_hid[...] = low
         e_gate[...] = by_gate
         e_up[...] = by_up
-        e_out[...] = jnp.dot(low, w_down[...], preferred_element_type=jnp.float32).astype(
-            e_out.dtype
-        )
+        result = jnp.dot(low, w_down[...], preferred_element_type=jnp.float32).astype(e_out.dtype)
+        e_out[...] = result
+        taken[here] = result
+
+    @pl.when(step >= tiles + e_tiles)
+    def _():
+        tile, tokens = x.shape[0], slots.shape[2]
+        at = step - tiles - e_tiles
+        here = pl.ds(pl.multiple_of(at * tile, tile), tile)
+        whole = mul(hid_all[here], down[...], 1, 1)
+        sig = stats_all[here][:, spare + experts : spare + experts + 1]
+        for b in range(slots.shape[1]):
+            span = slice(b * tokens, (b + 1) * tokens)
+            own = pl.ds(pl.multiple_of(at * size + b * capacity, capacity), capacity)
+            pick = chosen(slots[0, b : b + 1], capacity)
+            weighted = (share_all[own] * taken[own].astype(jnp.float32)).astype(jnp.bfloat16)
+            part[span] = (sig[span] * whole[span] + mul(pick, weighted, 0, 0)).astype(part.dtype)
 
     total = pl.num_programs(0)
-    times = (3, 8, 9, 10, 11)
+    times = (3, 8, 10, 12, 15)
     for i, action in enumerate(comm[1:-1]):
         at = jnp.minimum(times[min(i, len(times) - 1)], total - 1)
 
@@ -1182,19 +1208,34 @@
 
     def after(*shape):
         rest = (0,) * (len(shape) - 1)
-        return pl.BlockSpec(shape, lambda i: (jnp.maximum(i - tiles, 0),) + rest)
+        return pl.BlockSpec(
+            shape, lambda i: (jnp.clip(i - tiles, 0, e_rows // e_tile - 1),) + rest
+        )
+
+    e_tiles = e_rows // e_tile
+
+    def twice(*shape):
+        rest = (0,) * (len(shape) - 1)
+
+        def index(i):
+            return (jnp.where(i < tiles, i, jnp.maximum(i - tiles - e_tiles, 0)),) + rest
+        return pl.BlockSpec(shape, index)
+
+    def final(*shape):
+        rest = (0,) * (len(shape) - 1)
+        return pl.BlockSpec(shape, lambda i: (jnp.maximum(i - tiles - e_tiles, 0),) + rest)
 
     hbm = pl.BlockSpec(memory_space=pl.ANY)
     low, wide = jnp.bfloat16, jnp.float32
     sems = (11, levels, 1)
     return pl.pallas_call(
         functools.partial(forward_kernel, levels, capacity, experts, spare, tiles),
-        grid=(tiles + e_rows // e_tile,),
+        grid=(2 * tiles + e_tiles,),
         in_specs=[
             early(tile, width),
             resident(parts.shape),
             resident(extra.shape),
-            early(1, per, tokens),
+            twice(1, per, tokens),
             resident(w_gu.shape),
             resident(w_down.shape),
             hbm,
@@ -1211,6 +1252,8 @@
             after(e_tile, units),
             after(e_tile, units),
             after(e_tile, width),
+            early(per * capacity, 1),
+            final(tile, width),
             hbm,
         ],
         out_shape=[
@@ -1225,67 +1268,27 @@
             jax.ShapeDtypeStruct((e_rows, units), wide),
             jax.ShapeDtypeStruct((e_rows, units), wide),
             jax.ShapeDtypeStruct((e_rows, width), low),
+            jax.ShapeDtypeStruct((e_rows, 1), wide),
+            jax.ShapeDtypeStruct((rows, width), low),
             jax.ShapeDtypeStruct((count,) + late.shape, late.dtype),
         ],
         scratch_shapes=[
             pltpu.VMEM((e_rows, width), low),
+            pltpu.VMEM((rows, PAIR), low),
+            pltpu.VMEM((rows, PAIR - SIDE), wide),
+            pltpu.VMEM((e_rows, 1), wide),
             pltpu.SemaphoreType.DMA((1,)),
             pltpu.SemaphoreType.DMA(sems),
             pltpu.SemaphoreType.DMA(sems),
         ],
         compiler_params=pltpu.CompilerParams(
-            collective_id=ident, has_side_effects=True, vmem_limit_bytes=60 * 2**20
+            collective_id=ident, has_side_effects=True, vmem_limit_bytes=67043328
         ),
         cost_estimate=cost(
             (rows, width, 2 * PAIR), (e_rows, width, 2 * units), (e_rows, units, width)
         ),
         name="forward",
     )(x, parts, extra, slots.reshape(count // per, per, tokens), w_gu, w_down, late)
-
-
-def rows_out_kernel(
-    capacity, lane, hid, w_down, stats, slots, share, routed, grad, out, dots
-):
-    tokens = slots.shape[2]
-    whole = mul(hid[...], w_down[...], 1, 1)
-    for b in range(slots.shape[1]):
-        span = slice(b * tokens, (b + 1) * tokens)
-        here = slice(b * capacity, (b + 1) * capacity)
-        part = whole[span]
-        pick = chosen(slots[0, b : b + 1], capacity)
-        weighted = (share[here] * routed[here].astype(jnp.float32)).astype(jnp.bfloat16)
-        spread = mul(pick, weighted, 0, 0)
-        out[span] = (stats[span, lane : lane + 1] * part + spread).astype(out.dtype)
-        inner = jnp.sum(grad[span].astype(jnp.float32) * part, axis=1, keepdims=True)
-        dots[span] = jnp.broadcast_to(inner, (tokens, dots.shape[1]))
-
-
-def rows_out(hid, w_down, stats, slots, share, routed, grad, capacity, lane):
-    count, tokens = slots.shape
-    rows, width = count * tokens, routed.shape[1]
-    per = 4
-    tile = per * tokens
-    return pl.pallas_call(
-        functools.partial(rows_out_kernel, capacity, lane),
-        grid=(rows // tile,),
-        in_specs=[
-            tiled(tile, PAIR),
-            resident(w_down.shape),
-            tiled(tile, stats.shape[1]),
-            stacked(per, tokens),
-            tiled(per * capacity, 1),
-            tiled(per * capacity, width),
-            tiled(tile, width),
-        ],
-        out_specs=[tiled(tile, width), tiled(tile, 128)],
-        out_shape=[
-            jax.ShapeDtypeStruct((rows, width), jnp.bfloat16),
-            jax.ShapeDtypeStruct((rows, 128), jnp.float32),
-        ],
-        compiler_params=params(),
-        cost_estimate=cost((rows, PAIR, width), (rows, capacity, width)),
-        name="rows_out",
-    )(hid, w_down, stats, slots.reshape(count // per, per, tokens), share, routed, grad)
 
 
 def expert_back_kernel(
@@ -1362,7 +1365,7 @@
 
 def rows_back_kernel(
     levels, capacity, lane, grad, x, stats, hid, to_gate, to_up, slots, din, weights, w_down, part,
-    out, grad_parts, own, sum_weights, sum_down, *scratch
+    out, grad_parts, own, dots, sum_weights, sum_down, *scratch
 ):
     step = pl.program_id(0)
     comm = scatter_steps(levels, part, own, *scratch)
@@ -1377,6 +1380,10 @@
         sum_down[...] = jnp.zeros_like(sum_down)
 
     low = (stats[:, lane : lane + 1] * grad[...].astype(jnp.float32)).astype(jnp.bfloat16)
+    inner = jnp.sum(
+        mul(grad[...], w_down[...], 1, 0) * hid[...].astype(jnp.float32), axis=1, keepdims=True
+    )
+    dots[...] = jnp.broadcast_to(inner, dots.shape)
     dhid = mul(low, w_down[...], 1, 0)
     dgate = (dhid * to_gate[...]).astype(jnp.bfloat16)
     dup = (dhid * to_up[...]).astype(jnp.bfloat16)
@@ -1433,11 +1440,17 @@
             resident(w_down.shape),
             pl.BlockSpec(memory_space=pl.ANY),
         ],
-        out_specs=[tiled(tile, width), resident(parts_shape), resident(part.shape[1:])],
+        out_specs=[
+            tiled(tile, width),
+            resident(parts_shape),
+            resident(part.shape[1:]),
+            tiled(tile, 128),
+        ],
         out_shape=[
             jax.ShapeDtypeStruct((rows, width), jnp.bfloat16),
             jax.ShapeDtypeStruct(parts_shape, jnp.bfloat16),
             jax.ShapeDtypeStruct(part.shape[1:], jnp.float32),
+            jax.ShapeDtypeStruct((rows, 128), jnp.float32),
         ],
         scratch_shapes=[
             pltpu.VMEM(weights.shape[::-1], jnp.float32),
@@ -1670,30 +1683,23 @@
     placed = placed.astype(jnp.float32)
     (
         shared_hid, shared_gate_by, shared_up_by, stats, received, slice_gu, slice_down,
-        expert_hid, gate_by, up_by, expert_out, grad_all,
+        expert_hid, gate_by, up_by, expert_out, share, ffn_part, grad_all,
     ) = forward(
         normed_all, parts, extra, slots, w_expert_gu[0], w_expert_down[0], grad_out,
         capacity, experts_all, spare, levels, 8,
     )
     grad_all = grad_all.reshape(-1, model_width)
-    mine = (jnp.arange(stats.shape[1], dtype=jnp.int32) == spare + me).astype(jnp.float32)
-    prob_mine = jnp.sum(stats * mine, axis=1).reshape(devices, 1, own_rows)
-    share = jnp.sum(placed * prob_mine, axis=2).reshape(-1, 1)
-    ffn_part, gate_dots = rows_out(
-        shared_hid, slice_down, stats, slots, share, expert_out, grad_all, capacity, gate_lane
-    )
-
     expert_dout, expert_dgu, expert_din, slot_dots = expert_back(
         grad_all, slots, share, expert_out, gate_by, up_by, w_expert_gu[0], w_expert_down[0], capacity
+    )
+    normed_part, grad_parts, ffn_own, gate_dots = rows_back(
+        grad_all, normed_all, stats, shared_hid, shared_gate_by, shared_up_by, slots,
+        expert_din, slice_gu, slice_down, ffn_part.reshape(devices, own_rows, model_width),
+        parts.shape, capacity, gate_lane, levels, 9,
     )
     row_dots = jnp.sum(placed * slot_dots[:, 0].reshape(devices, capacity, 1), axis=1)
     dots = jnp.stack([row_dots, gate_dots[:, 0].reshape(devices, own_rows)], axis=1)
     dots = lax.all_to_all(dots, both, split_axis=0, concat_axis=0, tiled=True)
-    normed_part, grad_parts, ffn_own = rows_back(
-        grad_all, normed_all, stats, shared_hid, shared_gate_by, shared_up_by, slots,
-        expert_din, slice_gu, slice_down, ffn_part.reshape(devices, own_rows, model_width),
-        parts.shape, capacity, gate_lane, levels, 9,
-    )
     grad_expert_gu, grad_expert_down = expert_weight_grads(
         received, expert_dgu, expert_hid, expert_dout
     )

time: 831 us -> 811 us (0.976)
  Pallas kernels: 694 us -> 683 us
    pallas_call x1 -> x0, Pallas kernels: 21.1 us -> none  [rows_out(): pl.pallas_call(functools.partial(rows_out_kernel, capacity, lane), grid=(...]
  transfers between devices with their start and end apart: 3 -> 3, of which waited for: 0 -> 0; matrix products, arithmetic and copies ran while one was open for 8% -> 8% of each run, Pallas kernels for 33% -> 23%
where the time goes in v2:
time: 811 us; the launch traced here: 801 us
  Pallas kernels  683 us (84%)
  local copies, waits for them, and re-layouts  41.8 us (5%)
  matrix products  34.1 us (4%)
  other arithmetic  26 us (3%)
  starting transfers between devices  13.9 us (2%)
    pallas_call x1, Pallas kernels, scatter_last(): pl.pallas_call(functools.partial(scatter_last_kernel, levels), out_shape=...  108 us
    pallas_call x1, Pallas kernels, gather_first(): pl.pallas_call(functools.partial(gather_first_kernel, levels), out_shape=...  97.3 us
    pallas_call x1, Pallas kernels, forward(): pl.pallas_call(functools.partial(forward_kernel, levels, capacity, expert...  92.5 us
    pallas_call x1, Pallas kernels, rows_back(): pl.pallas_call(functools.partial(rows_back_kernel, levels, capacity, lane...  91.9 us
    pallas_call x1, Pallas kernels, scatter_all(): pl.pallas_call(functools.partial(scatter_kernel, levels), out_shape=jax.S...  82.4 us
    pallas_call x1, Pallas kernels, gather_all(): pl.pallas_call(functools.partial(gather_kernel, levels, size), out_shape=...  78.5 us
    pallas_call x2, Pallas kernels, scatter_lanes(): pl.pallas_call(functools.partial(scatter_lanes_kernel, levels), out_shape...  49.6 us
    pallas_call x1, Pallas kernels, expert_back(): pl.pallas_call(functools.partial(expert_back_kernel, capacity), grid=(row...  33.8 us
  transfers between devices with their start and end apart: 3, of which 0 were waited for; matrix products, arithmetic and copies ran while one was open for 8% of the time, Pallas kernels for 23%

profile of v2, /device:TPU:0, one launch (start us, length us, event | category | flops | bytes accessed | tf_op | source)
XLA Modules:
  0.0 801.0 jit_solution(2115887882505100604)
XLA Ops:
  4.5 97.3 %gather_first.1 = (bf16[3,8,256,512]{3,2,1,0:T(8,128)(2,1)}, bf16[512,2048]{1,0:T(8,128)(2,1)}, bf16[4,128,2048]{2,1,0:T(8,128)(2,1)}) custom-call(bf16[3,256,512]{2,1,0:T(8,128)(2,1)} %qkv.1, bf16[512,256]{1,0:T(8,128)(2,1)} %wout.1, bf16[128,2048]{1,0:T(8,128)(2,1)} %fusion.17.rows), custom_call_target="tpu_custom_call" | custom-call | tf_op jit(solution)/shard_map/gather_first/pallas_call | solution.py:614
  105.4 4.8 all-to-all-start
  110.2 3.6 fusion.40
  126.6 4.9 fusion.5.part
  131.5 30.7 %scatter_lanes.2 = f32[128,2048]{1,0:T(8,128)} custom-call(f32[4,128,2048]{2,1,0:T(8,128)} %fusion.5.part), custom_call_target="tpu_custom_call" | custom-call | tf_op jit(solution)/shard_map/scatter_lanes/pallas_call | solution.py:761
  167.6 2.7 copy.106.parts
  170.3 78.5 %gather_all.1 = (bf16[32,128,2048]{2,1,0:T(8,128)(2,1)}, s32[32,16,128]{2,1,0:T(8,128)}) custom-call(bf16[128,2048]{1,0:T(8,128)(2,1)} %multiply_convert_fusion.1.refs_0_, s32[16,128]{1,0:T(8,128)} %scatter.4.refs_1_), custom_call_target="tpu_custom_call" | custom-call | tf_op jit(solution)/shard_map/gather_all/pallas_call | solution.py:250
  250.8 92.5 %forward.1 = (bf16[4096,256]{1,0:T(8,128)(2,1)}, f32[4096,256]{1,0:T(8,128)}, f32[4096,256]{1,0:T(8,128)}, f32[4096,128]{1,0:T(8,128)}, bf16[1024,2048]{1,0:T(8,...) custom-call(bf16[4096,2048]{1,0:T(8,128)(2,1)} %bitcast.170, ...), custom_call_target="tpu_custom_call" | custom-call | flops 26306674688 | bytes 57409536 | tf_op jit(solution)/shard_map/forward/pallas_call | solution.py:1231
  343.3 33.8 %expert_back.1 = (bf16[1024,2048]{1,0:T(8,128)(2,1)}, bf16[2,1024,1408]{2,1,0:T(8,128)(2,1)}, bf16[1024,2048]{1,0:T(8,128)(2,1)}, f32[1024,128]{1,0:T(8,128)}) custom-call(bf16[4096,2048]{1,0:T(8,128)(2,1)} %bitcast.184, s32[4,8,128]{2,1,0:T(8,128)} %bitcast.159, f32[1024,1]{1,0:T(8,128)} %get-tuple-element.81.share, ...), custom_call_target="tpu_custom_call" | custom-call | flops 17716740096 | bytes 34340864 | tf_op jit(solution)/shard_map/expert_back/pallas_call | solution.py:1326
  377.1 91.9 %rows_back.1 = (bf16[4096,2048]{1,0:T(8,128)(2,1)}, bf16[8,3,256,176]{3,2,1,0:T(8,128)(2,1)}, f32[128,2048]{1,0:T(8,128)}, f32[4096,128]{1,0:T(8,128)}) custom-call(bf16[4096,2048]{1,0:T(8,128)(2,1)} %bitcast.185, bf16[4096,2048]{1,0:T(8,128)(2,1)} %bitcast.171, f32[4096,128]{1,0:T(8,128)} %get-tuple-element.77.stats, ...), custom_call_target="tpu_custom_call" | custom-call | flops 25769803776 | bytes 85983232 | tf_op jit(solution)/shard_map/rows_back/pallas_call | solution.py:1427
  472.5 4.3 all-to-all-start.1
  476.9 19.2 %expert_gu_grad.1 = f32[2,2048,1408]{2,1,0:T(8,128)} custom-call(bf16[1024,2048]{1,0:T(8,128)(2,1)} %get-tuple-element.101.x, bf16[2,1024,1408]{2,1,0:T(8,128)(2,1)} %get-tuple-element.102.dgu), custom_call_target="tpu_custom_call" | custom-call | flops 11811160064 | bytes 21495808 | tf_op jit(solution)/shard_map/expert_gu_grad/pallas_call | solution.py:1489
  496.0 13.1 %expert_down_grad.1 = f32[1408,2048]{1,0:T(8,128)} custom-call(bf16[1024,1408]{1,0:T(8,128)(2,1)} %get-tuple-element.103.hid, bf16[1024,2048]{1,0:T(8,128)(2,1)} %get-tuple-element.104.dout), custom_call_target="tpu_custom_call" | custom-call | flops 5905580032 | bytes 12845056 | tf_op jit(solution)/shard_map/expert_down_grad/pallas_call | solution.py:1499
  509.2 82.4 %scatter_all.1 = f32[128,2048]{1,0:T(8,128)} custom-call(bf16[32,128,2048]{2,1,0:T(8,128)(2,1)} %bitcast.123), custom_call_target="tpu_custom_call" | custom-call | tf_op jit(solution)/shard_map/scatter_all/pallas_call | solution.py:484
  591.6 2.6 copy.116
  594.3 4.7 all-to-all-start.2
  605.0 16.7 %gather_lanes.1 = bf16[4,128,2048]{2,1,0:T(8,128)(2,1)} custom-call(bf16[128,2048]{1,0:T(8,128)(2,1)} %fusion.39.rows), custom_call_target="tpu_custom_call" | custom-call | tf_op jit(solution)/shard_map/gather_lanes/pallas_call | solution.py:680
  621.7 3.0 convolution_convert_fusion.4
  635.5 2.6 add_convert_fusion
  638.1 18.9 %scatter_lanes.3 = f32[128,2048]{1,0:T(8,128)} custom-call(bf16[4,128,2048]{2,1,0:T(8,128)(2,1)} %bitcast.128), custom_call_target="tpu_custom_call" | custom-call | tf_op jit(solution)/shard_map/scatter_lanes/pallas_call | solution.py:761
  663.5 3.1 convolution_convert_fusion.1
  672.3 3.1 pad_maximum_fusion.qkv
  677.1 4.5 copy.117.parts
  681.6 107.9 %scatter_last.1 = (f32[3,256,512]{2,1,0:T(8,128)S(1)}, f32[512,256]{1,0:T(8,128)S(1)}, f32[2,24,2048]{2,1,0:T(8,128)S(1)}, f32[2,256,1408]{2,1,0:T(8,128)}, f32[1408,256]{1,0:T(8,128)S(1)}) custom-call(bf16[3,8,256,512]{3,2,1,0:T(8,128)(2,1)} %pad_maximum_fusion.qkv, bf16[512,2048]{1,0:T(8,128)(2,1)} %convolution_convert_fusion.wout, ...), custom_call_target="tpu_custom_call" | custom-call | tf_op jit(solution)/shard_map/scatter_last/pallas_call | solution.py:997
  (209 shorter events, 71.7 us)
Async XLA Ops:
  0.6 101.2 %copy-start.36 = (bf16[2,256,1408]{2,1,0:T(8,128)(2,1)S(1)}, bf16[2,256,1408]{2,1,0:T(8,128)(2,1)}, u32[]{:S(2)}) copy-start(bf16[2,256,1408]{2,1,0:T(8,128)(2,1)} %param.24) | copy-start | bytes 4325380
  105.4 62.3 %all-to-all-start = ((bf16[8,3,256,176]{2,3,1,0:T(8,128)(2,1)}), bf16[8,3,256,176]{2,3,1,0:T(8,128)(2,1)S(1)}, u32[]{:S(2)}, u32[]{:S(2)}) async-start(bf16[8,3,256,176]{2,3,1,0:T(8,128)(2,1)} %copy.104), calls=%async_computation | async-start | bytes 4325376 | tf_op jit(solution)/shard_map/all_to_all | solution.py:1660
  119.0 4.4 copy-start.31
  131.5 30.7 %copy-start.50 = (f32[2048]{0:T(1024)S(1)}, f32[2048]{0:T(1024)}, u32[]{:S(2)}) copy-start(f32[2048]{0:T(1024)} %param.23) | copy-start | bytes 24580
  131.5 30.8 %copy-start.40 = (bf16[2048,32]{0,1:T(8,128)(2,1)S(1)}, bf16[2048,32]{0,1:T(8,128)(2,1)}, u32[]{:S(2)}) copy-start(bf16[2048,32]{0,1:T(8,128)(2,1)} %param.22) | copy-start | bytes 393220
  131.5 31.2 %copy-start.57 = (s32[128,4]{0,1:T(4,128)S(1)}, s32[128,4]{0,1:T(4,128)}, u32[]{:S(2)}) copy-start(s32[128,4]{0,1:T(4,128)} %param.28) | copy-start | bytes 6148
  162.3 4.4 copy-start.45
  165.7 4.6 copy-start.53
  472.5 121.8 %all-to-all-start.1 = ((f32[32,2,128]{2,1,0:T(2,128)}), f32[32,2,128]{2,1,0:T(2,128)S(1)}, u32[]{:S(2)}, u32[]{:S(2)}) async-start(f32[32,2,128]{2,1,0:T(2,128)} %copy.107), calls=%async_computation.1 | async-start | bytes 65536 | tf_op jit(solution)/shard_map/all_to_all | solution.py:1702
  509.2 82.5 %copy-start.28 = (bf16[8,3,256,176]{3,2,1,0:T(8,128)(2,1)S(1)}, bf16[8,3,256,176]{3,2,1,0:T(8,128)(2,1)}, u32[]{:S(2)}) copy-start(bf16[8,3,256,176]{3,2,1,0:T(8,128)(2,1)} %get-tuple-element.95) | copy-start | bytes 6488068
  594.2 7.1 copy-start.5
  594.2 7.1 copy-start.27
  594.2 7.1 copy-start.41
  594.2 7.1 copy-start.46
  594.2 7.1 copy-start.51
  594.2 7.1 copy-start.54
  594.3 82.9 %all-to-all-start.2 = ((bf16[8,3,256,176]{2,3,1,0:T(8,128)(2,1)}), bf16[8,3,256,176]{2,3,1,0:T(8,128)(2,1)}, u32[]{:S(2)}, u32[]{:S(2)}) async-start(bf16[8,3,256,176]{2,3,1,0:T(8,128)(2,1)} %copy.116), calls=%async_computation.2 | async-start | bytes 4325376 | tf_op jit(solution)/shard_map/all_to_all | solution.py:1711
  599.0 4.8 copy-start.34
  605.0 16.7 %copy-start.33 = (bf16[512,2048]{1,0:T(8,128)(2,1)S(1)}, bf16[512,2048]{1,0:T(8,128)(2,1)}, u32[]{:S(2)}) copy-start(bf16[512,2048]{1,0:T(8,128)(2,1)} %get-tuple-element.68) | copy-start | bytes 6291460
  629.3 5.8 copy-start.22
  638.1 18.9 %copy-start.13 = (bf16[128,2048]{1,0:T(8,128)(2,1)S(1)}, bf16[128,2048]{1,0:T(8,128)(2,1)}, u32[]{:S(2)}) copy-start(bf16[128,2048]{1,0:T(8,128)(2,1)} %multiply_convert_fusion.1.refs_0_) | copy-start | bytes 1572868
  659.2 3.7 copy-start.8
  659.2 3.7 copy-start.48
  659.3 3.7 copy-start.56
  (39 other events, 77.6 us)

commit v3 on v2

--- a/solution.py
+++ b/solution.py
@@ -494,8 +494,12 @@
     )(part)
 
 
-def lane_block(ref, index, width):
-    return ref.at[:, pl.ds(pl.multiple_of(index * width, width), width)]
+def lane_block(ref, index, width, rows):
+    return ref.at[rows, pl.ds(pl.multiple_of(index * width, width), width)]
+
+
+def halves(count):
+    return [pl.ds(0, count // 2), pl.ds(count // 2, count // 2)]
 
 
 def gather_first_kernel(
@@ -506,14 +510,15 @@
     top = levels - 1
     x_dev, y_dev, c_dev = place.device(x=1 - x), place.device(y=1 - y), place.device(c=1 - c)
     UP, DOWN, YN = range(3)
-    pieces = 4
+    pieces, last = 5, 4
     row_kind = pieces * 3
-    own_weights = [qkv.at[k] for k in range(3)] + [wout]
+    OVER_UP, OVER_DOWN = row_kind + 1, row_kind + 2
+    own_weights = [qkv.at[k] for k in range(3)] + [wout.at[r] for r in halves(wout.shape[0])]
 
     def weight_refs(level, yy):
         spot = level * 2 + yy
         return [qkv_all.at[k, spot] for k in range(3)] + [
-            lane_block(wout_all, spot, wout.shape[1])
+            lane_block(wout_all, spot, wout.shape[1], r) for r in halves(wout.shape[0])
         ]
 
     def copy(index, level, ref, dst, device):
@@ -550,7 +555,9 @@
     def _():
         send(DOWN, z, own_weights, place.device(z=z - 1))
 
-    send(YN, z, own_weights, y_dev)
+    send(YN, z, own_weights, y_dev, last)
+    for i in range(last):
+        send(YN, z, own_weights, y_dev, i)
 
     def row_ref(xx, cc):
         return rows_all.at[xx * 2 + cc]
@@ -571,7 +578,21 @@
     on = copy(row_kind, 2, row_ref(1 - x, c), row_ref(1 - x, c), c_dev)
     on.start()
 
-    def relay(kind, level, inner, target):
+    def over(kind, level, target):
+        ref = weight_refs(level, 1 - y)[last]
+        return copy(kind, level, ref, ref, target)
+
+    arrived(YN, z, last)
+
+    @pl.when(z < top)
+    def _():
+        over(OVER_UP, z, place.device(z=z + 1)).start()
+
+    @pl.when(z > 0)
+    def _():
+        over(OVER_DOWN, z, place.device(z=z - 1)).start()
+
+    def relay(kind, over_kind, level, inner, target):
         for i in range(pieces):
             arrived(kind, level, i)
 
@@ -579,16 +600,22 @@
             def _():
                 send(kind, level, weight_refs(level, y), target, i)
 
-            send(YN, level, weight_refs(level, y), y_dev, i)
+            if i != last:
+                send(YN, level, weight_refs(level, y), y_dev, i)
+        over(over_kind, level, c_dev).wait_recv()
+
+        @pl.when(inner)
+        def _():
+            over(over_kind, level, target).start()
 
     for t in range(1, levels):
         @pl.when(z - t >= 0)
         def _():
-            relay(UP, z - t, z < top, place.device(z=z + 1))
+            relay(UP, OVER_UP, z - t, z < top, place.device(z=z + 1))
 
         @pl.when(z + t <= top)
         def _():
-            relay(DOWN, z + t, z > 0, place.device(z=z - 1))
+            relay(DOWN, OVER_DOWN, z + t, z > 0, place.device(z=z - 1))
 
     for one in own:
         one.wait()
@@ -597,16 +624,20 @@
     for one in (to_x, to_c, on):
         one.wait_send()
     for level in range(levels):
-        arrived(YN, level)
-        sent(YN, level)
+        for i in range(last):
+            arrived(YN, level, i)
+            copy(YN * pieces + i, level, own_weights[i], own_weights[i], c_dev).wait_send()
 
         @pl.when((z < top) & (level <= z))
         def _():
             sent(UP, level)
+            over(OVER_UP, level, c_dev).wait_send()
 
         @pl.when((z > 0) & (level >= z))
         def _():
             sent(DOWN, level)
+            over(OVER_DOWN, level, c_dev).wait_send()
+    copy(YN * pieces + last, z, own_weights[last], own_weights[last], c_dev).wait_send()
 
 
 def gather_first(w_qkv, w_out, rows, levels, lanes, ident):
@@ -621,9 +652,9 @@
         in_specs=[pl.BlockSpec(memory_space=pltpu.VMEM)] * 3,
         out_specs=[pl.BlockSpec(memory_space=pl.ANY)] * 3,
         scratch_shapes=[
-            pltpu.SemaphoreType.DMA((5,)),
-            pltpu.SemaphoreType.DMA((13, levels)),
-            pltpu.SemaphoreType.DMA((13, levels)),
+            pltpu.SemaphoreType.DMA((6,)),
+            pltpu.SemaphoreType.DMA((18, levels)),
+            pltpu.SemaphoreType.DMA((18, levels)),
         ],
         compiler_params=pltpu.CompilerParams(collective_id=ident, has_side_effects=True),
         name="gather_first",
@@ -777,14 +808,15 @@
 
 def scatter_last_kernel(
     levels, qkv, wout, small, parts, qkv_out, wout_out, small_out, gu_out, down_out,
-    q_load, w_load, q_y, w_y, q_z, w_z, q_tx, w_tx, s_y, s_tx,
+    q_load, w_load, q_y, w_y, q_z, w_z, q_tx, w_tx, s_y, s_tx, over_sum,
     load_sem, y_send, y_recv, z_send, z_recv, s_send, s_recv,
 ):
     place = Place(levels)
     z, y, x, c = place.z, place.y, place.x, place.c
     top = levels - 1
     x_dev, y_dev, c_dev = place.device(x=1 - x), place.device(y=1 - y), place.device(c=1 - c)
-    out_width = w_y.shape[2]
+    out_width = w_y.shape[3]
+    upper, lower = halves(wout.shape[0])
 
     def remote(sends, recvs, where, ref, dst, device):
         return pltpu.make_async_remote_copy(
@@ -796,15 +828,20 @@
             device_id_type=MESH_ID,
         )
 
+    LOWER, OVER = 4, 5
+    order = (OVER, LOWER, 0, 1, 2, 3)
+
     def block(level, yy):
         spot = level * 2 + yy
-        return [qkv.at[k, spot] for k in range(3)] + [lane_block(wout, spot, out_width)]
+        return [qkv.at[k, spot] for k in range(3)] + [
+            lane_block(wout, spot, out_width, r) for r in (upper, lower)
+        ]
 
     def pieces(q, w, level):
-        return [q.at[level, k] for k in range(3)] + [w.at[level]]
+        return [q.at[level, k] for k in range(3)] + [w.at[level, k] for k in range(3)]
 
     def load(level, i):
-        ref = block(level, y)[i]
+        ref = block(level, 1 - y)[LOWER] if i == OVER else block(level, y)[i]
         dst = pieces(q_load, w_load, level)[i]
         return pltpu.make_async_copy(ref, dst, load_sem.at[i, level])
 
@@ -839,8 +876,9 @@
         action(z)
 
     def begin(level):
-        for i in range(4):
-            across(level, i).start()
+        for i in order:
+            if i < LOWER:
+                across(level, i).start()
             load(level, i).start()
 
     each_level(begin)
@@ -902,24 +940,28 @@
     def f32(ref, rows):
         return ref[rows].astype(jnp.float32)
 
+    def own_sum(level, i, rows):
+        value = f32(pieces(q_load, w_load, level)[i], rows)
+        return value + f32(pieces(q_y, w_y, level)[i], rows) if i < LOWER else value
+
+    def ready(level, i):
+        load(level, i).wait()
+        if i < LOWER:
+            across(level, i).wait_recv()
+
     def pass_on(level, kind, first, target, slot):
-        mine, theirs = pieces(q_load, w_load, level), pieces(q_y, w_y, level)
         ahead, results = pieces(q_z, w_z, level), pieces(q_tx, w_tx, level)
-        for i in range(4):
-            load(level, i).wait()
-            across(level, i).wait_recv()
+        for i in order:
+            ready(level, i)
 
             @pl.when(first)
             def _():
-                strips(results[i], lambda rows: f32(mine[i], rows) + f32(theirs[i], rows))
+                strips(results[i], lambda rows: own_sum(level, i, rows))
 
             @pl.when(jnp.logical_not(first))
             def _():
                 along(kind, level, level, c_dev, i).wait_recv()
-                strips(
-                    results[i],
-                    lambda rows: f32(mine[i], rows) + f32(theirs[i], rows) + f32(ahead[i], rows),
-                )
+                strips(results[i], lambda rows: own_sum(level, i, rows) + f32(ahead[i], rows))
             along(kind, level, slot, target, i).start()
 
     for t in range(levels - 1, 0, -1):
@@ -938,20 +980,23 @@
             s_last = remote(s_send, s_recv, 3, small_out.at[c], small_out.at[c], c_dev)
             s_last.start()
 
-    results = [qkv_out.at[k] for k in range(3)] + [wout_out]
-    mine, theirs = pieces(q_load, w_load, z), pieces(q_y, w_y, z)
-    for i in range(4):
-        load(z, i).wait()
-        across(z, i).wait_recv()
-        strips(results[i], lambda rows: f32(mine[i], rows) + f32(theirs[i], rows))
-    for kind, here, slot in ((0, z > 0, z), (1, z < top, levels)):
-        ahead = pieces(q_z, w_z, slot)
-
-        @pl.when(here)
-        def _():
-            for i in range(4):
+    results = [qkv_out.at[k] for k in range(3)] + [wout_out.at[upper], wout_out.at[lower], over_sum]
+    passed = remote(y_send, y_recv, (LOWER, 0), w_tx.at[z, 2], w_y.at[z, 1], y_dev)
+    for i in order:
+        ready(z, i)
+        strips(results[i], lambda rows: own_sum(z, i, rows))
+        for kind, here, slot in ((0, z > 0, z), (1, z < top, levels)):
+            @pl.when(here)
+            def _():
                 along(kind, z, slot, c_dev, i).wait_recv()
-                strips(results[i], lambda rows: results[i][rows] + f32(ahead[i], rows))
+                ahead = pieces(q_z, w_z, slot)[i]
+                strips(results[i], lambda rows: results[i][rows] + f32(ahead, rows))
+        if i == OVER:
+            strips(w_tx.at[z, 2], lambda rows: over_sum[rows])
+            passed.start()
+    passed.wait_recv()
+    strips(results[LOWER], lambda rows: results[LOWER][rows] + f32(w_y.at[z, 1], rows))
+    passed.wait_send()
 
     remote(s_send, s_recv, 3, small_out.at[1 - c], small_out.at[1 - c], c_dev).wait_recv()
     for one in (s_first, s_x, s_yy, s_last):
@@ -962,12 +1007,12 @@
 
         @pl.when(level > z)
         def _():
-            for i in range(4):
+            for i in order:
                 along(0, level, level, c_dev, i).wait_send()
 
         @pl.when(level < z)
         def _():
-            for i in range(4):
+            for i in order:
                 along(1, level, level, c_dev, i).wait_send()
 
         @pl.when((z < top) & (level <= z))
@@ -991,7 +1036,7 @@
     def pair(count):
         return [
             pltpu.VMEM((count, 3, depth, width), low),
-            pltpu.VMEM((count, out_rows, out_width), low),
+            pltpu.VMEM((count, 3, out_rows // 2, out_width), low),
         ]
 
     return pl.pallas_call(
@@ -1012,11 +1057,12 @@
         + [
             pltpu.VMEM((3,) + small.shape[1:], jnp.float32),
             pltpu.VMEM((2 + levels,) + small.shape[1:], jnp.float32),
-            pltpu.SemaphoreType.DMA((4, levels)),
-            pltpu.SemaphoreType.DMA((4, levels)),
-            pltpu.SemaphoreType.DMA((4, levels)),
-            pltpu.SemaphoreType.DMA((2, 4, levels)),
-            pltpu.SemaphoreType.DMA((2, 4, levels)),
+            pltpu.VMEM((out_rows // 2, out_width), jnp.float32),
+            pltpu.SemaphoreType.DMA((6, levels)),
+            pltpu.SemaphoreType.DMA((5, levels)),
+            pltpu.SemaphoreType.DMA((5, levels)),
+            pltpu.SemaphoreType.DMA((2, 6, levels)),
+            pltpu.SemaphoreType.DMA((2, 6, levels)),
             pltpu.SemaphoreType.DMA((4 + 2 * levels,)),
             pltpu.SemaphoreType.DMA((4 + 2 * levels,)),
         ],
@@ -1120,17 +1166,34 @@
     return pltpu.CompilerParams(vmem_limit_bytes=60 * 2**20)
 
 
+def weight_loads(w_gu, w_down, gu_here, down_here, sem):
+    return [
+        pltpu.make_async_copy(w_gu, gu_here, sem.at[0]),
+        pltpu.make_async_copy(w_down, down_here, sem.at[1]),
+    ]
+
+
 def forward_kernel(
     levels, capacity, experts, spare, tiles, x, parts, extra, slots, w_gu, w_down, late,
     hid, to_gate, to_up, stats, taken_out, weights, down, e_hid, e_gate, e_up, e_out, share, part,
-    late_all, taken, hid_all, stats_all, share_all, own_sem, send_sems, recv_sems,
+    late_all, taken, hid_all, stats_all, share_all, gu_here, down_here, load_sem,
+    own_sem, send_sems, recv_sems,
 ):
     step = pl.program_id(0)
     comm = gather_steps(levels, [late], [late_all], own_sem, send_sems, recv_sems)
 
+    loads = weight_loads(w_gu, w_down, gu_here, down_here, load_sem)
+
     @pl.when(step == 0)
     def _():
         comm[0]()
+        for load in loads:
+            load.start()
+
+    @pl.when(step == tiles)
+    def _():
+        for load in loads:
+            load.wait()
 
     size = slots.shape[1] * capacity
 
@@ -1154,14 +1217,14 @@
         tile = e_out.shape[0]
         here = pl.ds(pl.multiple_of((step - tiles) * tile, tile), tile)
         rows = taken[here]
-        gate = jnp.dot(rows, w_gu[0], preferred_element_type=jnp.float32)
-        up = jnp.dot(rows, w_gu[1], preferred_element_type=jnp.float32)
+        gate = jnp.dot(rows, gu_here[0], preferred_element_type=jnp.float32)
+        up = jnp.dot(rows, gu_here[1], preferred_element_type=jnp.float32)
         hidden, by_gate, by_up = swish_parts(gate, up)
         low = hidden.astype(e_hid.dtype)
         e_hid[...] = low
         e_gate[...] = by_gate
         e_up[...] = by_up
-        result = jnp.dot(low, w_down[...], preferred_element_type=jnp.float32).astype(e_out.dtype)
+        result = jnp.dot(low, down_here[...], preferred_element_type=jnp.float32).astype(e_out.dtype)
         e_out[...] = result
         taken[here] = result
 
@@ -1236,8 +1299,8 @@
             resident(parts.shape),
             resident(extra.shape),
             twice(1, per, tokens),
-            resident(w_gu.shape),
-            resident(w_down.shape),
+            hbm,
+            hbm,
             hbm,
         ],
         out_specs=[
@@ -1277,6 +1340,9 @@
             pltpu.VMEM((rows, PAIR), low),
             pltpu.VMEM((rows, PAIR - SIDE), wide),
             pltpu.VMEM((e_rows, 1), wide),
+            pltpu.VMEM(w_gu.shape, w_gu.dtype),
+            pltpu.VMEM(w_down.shape, w_down.dtype),
+            pltpu.SemaphoreType.DMA((2,)),
             pltpu.SemaphoreType.DMA((1,)),
             pltpu.SemaphoreType.DMA(sems),
             pltpu.SemaphoreType.DMA(sems),
@@ -1292,8 +1358,17 @@
 
 
 def expert_back_kernel(
-    capacity, grad, slots, share, out, to_gate, to_up, w_gu, w_down, dout, dgu, din, dots
+    capacity, grad, slots, share, out, to_gate, to_up, w_gu, w_down,
+    dout, dgu, din, dots, gu_here, down_here, load_sem,
 ):
+    loads = weight_loads(w_gu, w_down, gu_here, down_here, load_sem)
+    first = pl.program_id(0) == 0
+
+    @pl.when(first)
+    def _():
+        for load in loads[::-1]:
+            load.start()
+
     tokens = slots.shape[2]
     size = slots.shape[1]
     taken = []
@@ -1309,12 +1384,22 @@
     dots[...] = jnp.broadcast_to(inner, dots.shape)
     low = (share[...] * rows).astype(jnp.bfloat16)
     dout[...] = low
-    dhid = mul(low, w_down[...], 1, 1)
+
+    @pl.when(first)
+    def _():
+        loads[1].wait()
+
+    dhid = mul(low, down_here[...], 1, 1)
     dgate = (dhid * to_gate[...]).astype(jnp.bfloat16)
     dup = (dhid * to_up[...]).astype(jnp.bfloat16)
     dgu[0] = dgate
     dgu[1] = dup
-    din[...] = (mul(dgate, w_gu[0], 1, 1) + mul(dup, w_gu[1], 1, 1)).astype(din.dtype)
+
+    @pl.when(first)
+    def _():
+        loads[0].wait()
+
+    din[...] = (mul(dgate, gu_here[0], 1, 1) + mul(dup, gu_here[1], 1, 1)).astype(din.dtype)
 
 
 def expert_back(grad, slots, share, out, to_gate, to_up, w_gu, w_down, capacity):
@@ -1333,8 +1418,8 @@
             tiled(tile, width),
             tiled(tile, units),
             tiled(tile, units),
-            resident(w_gu.shape),
-            resident(w_down.shape),
+            pl.BlockSpec(memory_space=pl.ANY),
+            pl.BlockSpec(memory_space=pl.ANY),
         ],
         out_specs=[
             tiled(tile, width),
@@ -1347,6 +1432,11 @@
             jax.ShapeDtypeStruct((2, rows, units), jnp.bfloat16),
             jax.ShapeDtypeStruct((rows, width), jnp.bfloat16),
             jax.ShapeDtypeStruct((rows, 128), jnp.float32),
+        ],
+        scratch_shapes=[
+            pltpu.VMEM(w_gu.shape, w_gu.dtype),
+            pltpu.VMEM(w_down.shape, w_down.dtype),
+            pltpu.SemaphoreType.DMA((2,)),
         ],
         compiler_params=params(),
         cost_estimate=cost((rows, width, units), (rows, 2 * units, width)),

time: 811 us -> 804 us (level)
  no operation moved by 1% of the time
where the time goes in v3:
time: 804 us; the launch traced here: 794 us
  Pallas kernels  676 us (84%)
  local copies, waits for them, and re-layouts  41.8 us (5%)
  matrix products  34.1 us (4%)
  other arithmetic  26 us (3%)
  starting transfers between devices  13.9 us (2%)
    pallas_call x1, Pallas kernels, scatter_last(): pl.pallas_call(functools.partial(scatter_last_kernel, levels), out_shape=...  113 us
    pallas_call x1, Pallas kernels, rows_back(): pl.pallas_call(functools.partial(rows_back_kernel, levels, capacity, lane...  91.9 us
    pallas_call x1, Pallas kernels, gather_first(): pl.pallas_call(functools.partial(gather_first_kernel, levels), out_shape=...  89.2 us
    pallas_call x1, Pallas kernels, forward(): pl.pallas_call(functools.partial(forward_kernel, levels, capacity, expert...  87.3 us
    pallas_call x1, Pallas kernels, scatter_all(): pl.pallas_call(functools.partial(scatter_kernel, levels), out_shape=jax.S...  82.5 us
    pallas_call x1, Pallas kernels, gather_all(): pl.pallas_call(functools.partial(gather_kernel, levels, size), out_shape=...  78.5 us
    pallas_call x2, Pallas kernels, scatter_lanes(): pl.pallas_call(functools.partial(scatter_lanes_kernel, levels), out_shape...  49.7 us
    pallas_call x1, Pallas kernels, expert_back(): pl.pallas_call(functools.partial(expert_back_kernel, capacity), grid=(row...  34.9 us
  transfers between devices with their start and end apart: 3, of which 0 were waited for; matrix products, arithmetic and copies ran while one was open for 8% of the time, Pallas kernels for 23%

profile of v3, /device:TPU:0, one launch (start us, length us, event | category | flops | bytes accessed | tf_op | source)
XLA Modules:
  0.0 793.8 jit_solution(7463359475075245979)
XLA Ops:
  4.5 89.2 %gather_first.1 = (bf16[3,8,256,512]{3,2,1,0:T(8,128)(2,1)}, bf16[512,2048]{1,0:T(8,128)(2,1)}, bf16[4,128,2048]{2,1,0:T(8,128)(2,1)}) custom-call(bf16[3,256,512]{2,1,0:T(8,128)(2,1)} %qkv.1, bf16[512,256]{1,0:T(8,128)(2,1)} %wout.1, bf16[128,2048]{1,0:T(8,128)(2,1)} %fusion.17.rows), custom_call_target="tpu_custom_call" | custom-call | tf_op jit(solution)/shard_map/gather_first/pallas_call | solution.py:645
  97.3 4.9 all-to-all-start
  102.2 3.6 fusion.40
  118.5 4.9 fusion.5.part
  123.4 30.7 %scatter_lanes.2 = f32[128,2048]{1,0:T(8,128)} custom-call(f32[4,128,2048]{2,1,0:T(8,128)} %fusion.5.part), custom_call_target="tpu_custom_call" | custom-call | tf_op jit(solution)/shard_map/scatter_lanes/pallas_call | solution.py:792
  159.6 2.7 copy.106.parts
  162.3 78.5 %gather_all.1 = (bf16[32,128,2048]{2,1,0:T(8,128)(2,1)}, s32[32,16,128]{2,1,0:T(8,128)}) custom-call(bf16[128,2048]{1,0:T(8,128)(2,1)} %multiply_convert_fusion.1.refs_0_, s32[16,128]{1,0:T(8,128)} %scatter.4.refs_1_), custom_call_target="tpu_custom_call" | custom-call | tf_op jit(solution)/shard_map/gather_all/pallas_call | solution.py:250
  242.7 87.3 %forward.1 = (bf16[4096,256]{1,0:T(8,128)(2,1)}, f32[4096,256]{1,0:T(8,128)}, f32[4096,256]{1,0:T(8,128)}, f32[4096,128]{1,0:T(8,128)}, bf16[1024,2048]{1,0:T(8,...) custom-call(bf16[4096,2048]{1,0:T(8,128)(2,1)} %bitcast.170, ...), custom_call_target="tpu_custom_call" | custom-call | flops 26306674688 | bytes 57409536 | tf_op jit(solution)/shard_map/forward/pallas_call | solution.py:1294
  330.0 34.9 %expert_back.1 = (bf16[1024,2048]{1,0:T(8,128)(2,1)}, bf16[2,1024,1408]{2,1,0:T(8,128)(2,1)}, bf16[1024,2048]{1,0:T(8,128)(2,1)}, f32[1024,128]{1,0:T(8,128)}) custom-call(bf16[4096,2048]{1,0:T(8,128)(2,1)} %bitcast.184, s32[4,8,128]{2,1,0:T(8,128)} %bitcast.159, f32[1024,1]{1,0:T(8,128)} %get-tuple-element.81.share, ...), custom_call_target="tpu_custom_call" | custom-call | flops 17716740096 | bytes 34340864 | tf_op jit(solution)/shard_map/expert_back/pallas_call | solution.py:1411
  364.9 91.9 %rows_back.1 = (bf16[4096,2048]{1,0:T(8,128)(2,1)}, bf16[8,3,256,176]{3,2,1,0:T(8,128)(2,1)}, f32[128,2048]{1,0:T(8,128)}, f32[4096,128]{1,0:T(8,128)}) custom-call(bf16[4096,2048]{1,0:T(8,128)(2,1)} %bitcast.185, bf16[4096,2048]{1,0:T(8,128)(2,1)} %bitcast.171, f32[4096,128]{1,0:T(8,128)} %get-tuple-element.77.stats, ...), custom_call_target="tpu_custom_call" | custom-call | flops 25769803776 | bytes 85983232 | tf_op jit(solution)/shard_map/rows_back/pallas_call | solution.py:1517
  460.3 4.3 all-to-all-start.1
  464.6 19.2 %expert_gu_grad.1 = f32[2,2048,1408]{2,1,0:T(8,128)} custom-call(bf16[1024,2048]{1,0:T(8,128)(2,1)} %get-tuple-element.101.x, bf16[2,1024,1408]{2,1,0:T(8,128)(2,1)} %get-tuple-element.102.dgu), custom_call_target="tpu_custom_call" | custom-call | flops 11811160064 | bytes 21495808 | tf_op jit(solution)/shard_map/expert_gu_grad/pallas_call | solution.py:1579
  483.8 13.1 %expert_down_grad.1 = f32[1408,2048]{1,0:T(8,128)} custom-call(bf16[1024,1408]{1,0:T(8,128)(2,1)} %get-tuple-element.103.hid, bf16[1024,2048]{1,0:T(8,128)(2,1)} %get-tuple-element.104.dout), custom_call_target="tpu_custom_call" | custom-call | flops 5905580032 | bytes 12845056 | tf_op jit(solution)/shard_map/expert_down_grad/pallas_call | solution.py:1589
  496.9 82.5 %scatter_all.1 = f32[128,2048]{1,0:T(8,128)} custom-call(bf16[32,128,2048]{2,1,0:T(8,128)(2,1)} %bitcast.123), custom_call_target="tpu_custom_call" | custom-call | tf_op jit(solution)/shard_map/scatter_all/pallas_call | solution.py:484
  579.4 2.6 copy.116
  582.1 4.7 all-to-all-start.2
  592.8 16.6 %gather_lanes.1 = bf16[4,128,2048]{2,1,0:T(8,128)(2,1)} custom-call(bf16[128,2048]{1,0:T(8,128)(2,1)} %fusion.39.rows), custom_call_target="tpu_custom_call" | custom-call | tf_op jit(solution)/shard_map/gather_lanes/pallas_call | solution.py:711
  609.5 3.0 convolution_convert_fusion.4
  623.2 2.6 add_convert_fusion
  625.8 19.0 %scatter_lanes.3 = f32[128,2048]{1,0:T(8,128)} custom-call(bf16[4,128,2048]{2,1,0:T(8,128)(2,1)} %bitcast.128), custom_call_target="tpu_custom_call" | custom-call | tf_op jit(solution)/shard_map/scatter_lanes/pallas_call | solution.py:792
  651.3 3.1 convolution_convert_fusion.1
  660.1 3.1 pad_maximum_fusion.qkv
  665.0 4.5 copy.117.parts
  669.4 112.9 %scatter_last.1 = (f32[3,256,512]{2,1,0:T(8,128)S(1)}, f32[512,256]{1,0:T(8,128)S(1)}, f32[2,24,2048]{2,1,0:T(8,128)S(1)}, f32[2,256,1408]{2,1,0:T(8,128)}, f32[1408,256]{1,0:T(8,128)S(1)}) custom-call(bf16[3,8,256,512]{3,2,1,0:T(8,128)(2,1)} %pad_maximum_fusion.qkv, bf16[512,2048]{1,0:T(8,128)(2,1)} %convolution_convert_fusion.wout, ...), custom_call_target="tpu_custom_call" | custom-call | tf_op jit(solution)/shard_map/scatter_last/pallas_call | solution.py:1042
  (209 shorter events, 71.7 us)
Async XLA Ops:
  0.6 93.2 %copy-start.36 = (bf16[2,256,1408]{2,1,0:T(8,128)(2,1)S(1)}, bf16[2,256,1408]{2,1,0:T(8,128)(2,1)}, u32[]{:S(2)}) copy-start(bf16[2,256,1408]{2,1,0:T(8,128)(2,1)} %param.24) | copy-start | bytes 4325380
  97.3 62.3 %all-to-all-start = ((bf16[8,3,256,176]{2,3,1,0:T(8,128)(2,1)}), bf16[8,3,256,176]{2,3,1,0:T(8,128)(2,1)S(1)}, u32[]{:S(2)}, u32[]{:S(2)}) async-start(bf16[8,3,256,176]{2,3,1,0:T(8,128)(2,1)} %copy.104), calls=%async_computation | async-start | bytes 4325376 | tf_op jit(solution)/shard_map/all_to_all | solution.py:1750
  111.0 4.4 copy-start.31
  123.4 30.7 %copy-start.50 = (f32[2048]{0:T(1024)S(1)}, f32[2048]{0:T(1024)}, u32[]{:S(2)}) copy-start(f32[2048]{0:T(1024)} %param.23) | copy-start | bytes 24580
  123.4 30.8 %copy-start.40 = (bf16[2048,32]{0,1:T(8,128)(2,1)S(1)}, bf16[2048,32]{0,1:T(8,128)(2,1)}, u32[]{:S(2)}) copy-start(bf16[2048,32]{0,1:T(8,128)(2,1)} %param.22) | copy-start | bytes 393220
  123.4 31.2 %copy-start.57 = (s32[128,4]{0,1:T(4,128)S(1)}, s32[128,4]{0,1:T(4,128)}, u32[]{:S(2)}) copy-start(s32[128,4]{0,1:T(4,128)} %param.28) | copy-start | bytes 6148
  154.3 4.4 copy-start.45
  157.7 4.6 copy-start.53
  460.3 121.8 %all-to-all-start.1 = ((f32[32,2,128]{2,1,0:T(2,128)}), f32[32,2,128]{2,1,0:T(2,128)S(1)}, u32[]{:S(2)}, u32[]{:S(2)}) async-start(f32[32,2,128]{2,1,0:T(2,128)} %copy.107), calls=%async_computation.1 | async-start | bytes 65536 | tf_op jit(solution)/shard_map/all_to_all | solution.py:1792
  496.9 82.5 %copy-start.28 = (bf16[8,3,256,176]{3,2,1,0:T(8,128)(2,1)S(1)}, bf16[8,3,256,176]{3,2,1,0:T(8,128)(2,1)}, u32[]{:S(2)}) copy-start(bf16[8,3,256,176]{3,2,1,0:T(8,128)(2,1)} %get-tuple-element.95) | copy-start | bytes 6488068
  582.0 7.1 copy-start.5
  582.0 7.1 copy-start.27
  582.1 7.1 copy-start.41
  582.1 7.1 copy-start.46
  582.1 7.1 copy-start.51
  582.1 7.1 copy-start.54
  582.1 82.9 %all-to-all-start.2 = ((bf16[8,3,256,176]{2,3,1,0:T(8,128)(2,1)}), bf16[8,3,256,176]{2,3,1,0:T(8,128)(2,1)}, u32[]{:S(2)}, u32[]{:S(2)}) async-start(bf16[8,3,256,176]{2,3,1,0:T(8,128)(2,1)} %copy.116), calls=%async_computation.2 | async-start | bytes 4325376 | tf_op jit(solution)/shard_map/all_to_all | solution.py:1801
  586.8 4.8 copy-start.34
  592.8 16.6 %copy-start.33 = (bf16[512,2048]{1,0:T(8,128)(2,1)S(1)}, bf16[512,2048]{1,0:T(8,128)(2,1)}, u32[]{:S(2)}) copy-start(bf16[512,2048]{1,0:T(8,128)(2,1)} %get-tuple-element.68) | copy-start | bytes 6291460
  617.1 5.8 copy-start.22
  625.8 19.0 %copy-start.13 = (bf16[128,2048]{1,0:T(8,128)(2,1)S(1)}, bf16[128,2048]{1,0:T(8,128)(2,1)}, u32[]{:S(2)}) copy-start(bf16[128,2048]{1,0:T(8,128)(2,1)} %multiply_convert_fusion.1.refs_0_) | copy-start | bytes 1572868
  647.0 3.7 copy-start.8
  647.1 3.7 copy-start.48
  647.1 3.7 copy-start.56
  (39 other events, 77.6 us)
